TPU v7x, 32 devices: a whole 2x2x4 slice. The times are simulated.
32 devices in a mesh: grp: 2 (over y), shot: 4 (over x, core), slab: 4 (over z).
Axes of the slice: x: 2, y: 2, z: 4, core: 2. Of those that a mesh axis runs over, the one named last changes fastest.
Arguments:
- courant_sq: float32 [512, 1024], P(('grp', 'slab')), parts along dimension 0, may hold values from 0.05 to 0.25
- sponge_level: int32 [512, 1024], P(('grp', 'slab')), parts along dimension 0, may hold values from 0 to 3
- source_later: float32 [16, 256, 1024], P(('grp', 'shot'), 'slab'), parts along dimension 0, may hold values from -6 to 6
- source_now: float32 [16, 256, 1024], P(('grp', 'shot'), 'slab'), parts along dimension 0, may hold values from -6 to 6
- receiver_later: float32 [16, 256, 1024], P(('grp', 'shot'), 'slab'), parts along dimension 0, may hold values from -6 to 6
- receiver_now: float32 [16, 256, 1024], P(('grp', 'shot'), 'slab'), parts along dimension 0, may hold values from -6 to 6
- traces: float32 [16, 16, 512], P(('grp', 'shot')), parts along dimension 0, may hold values from -24 to 24
- wavelet: float32 [512], P('grp'), parts along dimension 0, may hold values from -24 to 24
- source_depth: int32 [16], P(('grp', 'shot')), parts along dimension 0, may hold values from 0 to 255
- source_lateral: int32 [16], P(('grp', 'shot')), parts along dimension 0, may hold values from 0 to 1023
- receiver_depth: int32 [16, 512], P(('grp', 'shot')), parts along dimension 0, may hold values from 0 to 255
- receiver_lateral: int32 [16, 512], P(('grp', 'shot')), parts along dimension 0, may hold values from 0 to 1023
- checkpoint_step: int32 [16], P(('grp', 'shot')), parts along dimension 0, may hold values from 0 to 240
Outputs:
- image: float32 [512, 1024], P(('grp', 'slab')), parts along dimension 0
- source_out: float32 [16, 256, 1024], P(('grp', 'shot'), 'slab'), parts along dimension 0
- receiver_out: float32 [16, 256, 1024], P(('grp', 'shot'), 'slab'), parts along dimension 0
There are 2 independent parts, one for each index of `grp`. A program takes and returns all parts, laid end to end along the dimension named above; each array names one. Nothing has to cross between parts.
All inputs are finite; a program needn't handle non-finite values.
Results may differ from a plain program's by a relative error of at most 0.0003.
Values sent between devices are 32-bit elements; how exact they have to be, the bound alone decides.
A program may use at most 64 MiB of HBM per device.

v0:
```python
import math
import jax
import jax.numpy as jnp
from jax import lax
from jax.sharding import PartitionSpec as P

STEPS = 16
stencil_coeffs = (-205.0 / 72.0, 8.0 / 5.0, -1.0 / 5.0, 8.0 / 315.0, -1.0 / 560.0)


def extended_2(cells, sides, width):
    for axis, dim in sides:
        count = lax.axis_size(axis)
        ends = count - 1
        head = lax.slice_in_dim(cells, 0, width, axis=dim)
        tail = lax.slice_in_dim(cells, cells.shape[dim] - width, cells.shape[dim], axis=dim)
        cells = jnp.concatenate(
            [
                lax.ppermute(tail, axis, [(i, (i + 1) % count) for i in range(ends)]),
                cells,
                lax.ppermute(head, axis, [((i + 1) % count, i) for i in range(ends)]),
            ],
            axis=dim,
        )
    return cells


def laplace(extended):
    row_count = extended.shape[-2] - 8
    width = extended.shape[-1]
    centre = extended[..., 4 : 4 + row_count, :]
    pad_spec = [(0, 0)] * (centre.ndim - 1) + [(4, 4)]
    padded = jnp.pad(centre, pad_spec)
    result = 2.0 * stencil_coeffs[0] * centre
    for offset in range(1, 5):
        result = result + stencil_coeffs[offset] * (
            extended[..., 4 + offset : 4 + offset + row_count, :]
            + extended[..., 4 - offset : 4 - offset + row_count, :]
            + padded[..., 4 + offset : 4 + offset + width]
            + padded[..., 4 - offset : 4 - offset + width]
        )
    return result


def local(
    courant_sq,
    sponge_level,
    source_later,
    source_now,
    receiver_later,
    receiver_now,
    traces,
    wavelet,
    source_depth,
    source_lateral,
    receiver_depth,
    receiver_lateral,
    checkpoint_step,
):
    slab_rows = courant_sq.shape[0]
    lateral_cells = courant_sq.shape[1]
    first_row = lax.axis_index("slab") * slab_rows
    damping = 1.0 - 0.06 * sponge_level.astype(jnp.float32)
    lateral_ids = jnp.arange(lateral_cells, dtype=jnp.int32)
    lateral_table = (receiver_lateral[:, :, None] == lateral_ids[None, None, :]).astype(jnp.float32)
    source_column = lateral_ids[None, :] == source_lateral[:, None]

    def advance(src_now, src_hi, rec_now, rec_hi, laplacian, velocity, damper, top_row, step_index):
        row_count = src_now.shape[1]
        row_ids = top_row + jnp.arange(row_count, dtype=jnp.int32)
        pulse = wavelet[checkpoint_step + STEPS - 1 - step_index]
        source_cell = (row_ids[None, :, None] == source_depth[:, None, None]) & source_column[
            :, None, :
        ]
        injected_src = jnp.where(source_cell, pulse[:, None, None], 0.0)
        src_next = 2.0 * src_now - src_hi + velocity * laplacian[0] - velocity * injected_src
        trace_now = lax.dynamic_index_in_dim(traces, step_index, 1, keepdims=False)
        depth_table = jnp.where(
            row_ids[None, :, None] == receiver_depth[:, None, :], trace_now[:, None, :], 0.0
        )
        injected_rec = jnp.einsum(
            "szr,srx->szx",
            depth_table,
            lateral_table,
            precision=lax.Precision.HIGHEST,
            preferred_element_type=jnp.float32,
        )
        rec_next = 2.0 * rec_now - rec_hi + velocity * laplacian[1] + velocity * injected_rec
        rec_next = damper * rec_next
        return (src_next, rec_next)

    start_image = jnp.zeros(courant_sq.shape, jnp.float32)
    model = extended_2(jnp.stack([courant_sq, damping]), (("slab", 1),), 8)
    velocity_wide = model[0, 4 : slab_rows + 12]
    damper_wide = model[1, 4 : slab_rows + 12]

    def pair_step(pair_index, carry):
        src_hi, src_now, rec_hi, rec_now, image_local = carry
        step_first = 2 * pair_index
        image_local = image_local + jnp.sum(src_now * rec_now, axis=0)
        extended = extended_2(jnp.stack([src_now, rec_now, src_hi, rec_hi]), (("slab", 2),), 8)
        laplacian = laplace(extended[0:2])
        src_wide = extended[0, :, 4 : slab_rows + 12]
        rec_wide = extended[1, :, 4 : slab_rows + 12]
        src_hi_wide = extended[2, :, 4 : slab_rows + 12]
        rec_hi_wide = extended[3, :, 4 : slab_rows + 12]
        src_mid, rec_mid = advance(
            src_wide,
            src_hi_wide,
            rec_wide,
            rec_hi_wide,
            laplacian,
            velocity_wide,
            damper_wide,
            first_row - 4,
            step_first,
        )
        src_centre = src_mid[:, 4 : slab_rows + 4]
        rec_centre = rec_mid[:, 4 : slab_rows + 4]
        image_local = image_local + jnp.sum(src_centre * rec_centre, axis=0)
        second = laplace(jnp.stack([src_mid, rec_mid]))
        src_last, rec_last = advance(
            src_centre,
            src_now,
            rec_centre,
            rec_now,
            second,
            courant_sq,
            damping,
            first_row,
            step_first + 1,
        )
        return (src_centre, src_last, rec_centre, rec_last, image_local)

    carry = lax.fori_loop(
        0,
        STEPS // 2,
        pair_step,
        (source_later, source_now, receiver_later, receiver_now, start_image),
    )
    source_final = carry[1]
    receiver_final = carry[3]
    image_total = lax.psum(carry[4], "shot")
    shots_all = lax.axis_size("shot") * source_now.shape[0]
    image = image_total / math.sqrt(STEPS * shots_all)
    return (image, source_final, receiver_final)


def solution(mesh):
    in_specs = (
        P(("grp", "slab"), None),
        P(("grp", "slab"), None),
        P(("grp", "shot"), "slab", None),
        P(("grp", "shot"), "slab", None),
        P(("grp", "shot"), "slab", None),
        P(("grp", "shot"), "slab", None),
        P(("grp", "shot"), None, None),
        P("grp"),
        P(("grp", "shot")),
        P(("grp", "shot")),
        P(("grp", "shot"), None),
        P(("grp", "shot"), None),
        P(("grp", "shot")),
    )
    out_specs = (
        P(("grp", "slab"), None),
        P(("grp", "shot"), "slab", None),
        P(("grp", "shot"), "slab", None),
    )
    return jax.shard_map(local, mesh=mesh, in_specs=in_specs, out_specs=out_specs, check_vma=False)
```

profile of v0, /device:TPU:0, one launch (start us, length us, event | category | flops | bytes accessed | tf_op | source)
XLA Modules:
  0.0 274.1 jit_solution(1386798049830185891)
XLA Ops:
  7.2 0.9 copy-done.11
  9.0 5.1 %collective-permute-start.2 = (f32[2,8,1024]{2,1,0:T(8,128)S(1)}, f32[2,8,1024]{2,1,0:T(8,128)S(1)}, u32[]{:S(2)}, u32[]{:S(2)}) collective-permute-start(f32[2,8,1024]{2,1,0:T(8,128)S(1)} %get-tuple-element.729), channel_id=1, source_target_pairs={{0,1},{1,2},{2,3},{4,5},{5,6},{6,7},{8,9},{9,10},{10,11},{12,13},{... | collective-permute-start | bytes 196616 | tf_op jit(solution)/shard_map/ppermute | solution.py:19
  14.1 1.3 collective-permute-start.3
  16.0 4.3 %collective-permute-done.3 = f32[2,8,1024]{2,1,0:T(8,128)S(1)} collective-permute-done((f32[2,8,1024]{2,1,0:T(8,128)S(1)}, f32[2,8,1024]{2,1,0:T(8,128)S(1)}, u32[]{:S(2)}, u32[]{:S(2)}) %collective-permute-start.3) | collective-permute-done | bytes 65568 | tf_op jit(solution)/shard_map/ppermute | solution.py:21
  21.1 209.0 %while.26 = (s32[]{:T(128)}, f32[2,64,1024]{2,1,0:T(8,128)S(1)}, f32[2,64,1024]{2,1,0:T(8,128)S(1)}, f32[2,64,1024]{2,1,0:T(8,128)S(1)}, f32[2,64,1024]{2,1,0:T(...) while((s32[]{:T(128)}, f32[2,64,1024]{2,1,0:T(8,128)S(1)}, ...), condition=%wide.region_3.4_spmd.clone, body=%wide.region_0.3_spmd.clone.sunk | while | flops 1741394304 | bytes 51560036 | solution.py:135
  21.1 0.8 pad_maximum_fusion.22
  21.9 1.3 collective-permute-start
  23.2 4.6 %collective-permute-start.1 = (f32[4,2,8,1024]{3,2,1,0:T(8,128)}, f32[4,2,8,1024]{3,2,1,0:T(8,128)S(1)}, u32[]{:S(2)}, u32[]{:S(2)}) collective-permute-start(f32[4,2,8,1024]{3,2,1,0:T(8,128)} %get-tuple-element.863), channel_id=1, source_target_pairs={{0,1},{1,2},{2,3},{4,5},{5,6},{6,7},{8,9},{9,10},{10,11},{12,13},{... | collective-permute-start | bytes 786440 | tf_op jit(solution)/shard_map/while/body/eval_jaxpr/ppermute | solution.py:19
  30.7 1.3 collective-permute-done.1
  32.3 2.6 fusion.117
  35.9 3.2 %fusion.118 = f32[2,72,1024]{2,1,0:T(8,128)S(1)} fusion(f32[2,2,72,1024]{3,2,1,0:T(8,128)S(1)} %fusion.117, f32[4,2,80,1024]{3,2,1,0:T(8,128)S(1)} %pad_maximum_fusion.23, s32[2,512]{1,0:T(2,128)S(1)} %copy-done.17, f32[72,1024]{1,0:T(8,128)S(1)} %bitcast.101, f32[72,1024]{1,0:T(8,128)S(1)} %bitcast.98, f32[2,512]{1,0:T(2,128)S(1)} %get-tuple-element.864, ...), kind=kOutput, calls=%fused_computation.109.clone.1 | convolution fusion | flops 909246464 | bytes 2961696 | tf_op jit(solution)/shard_map/while/body/eval_jaxpr/szr,srx->szx/dot_general | solution.py:81
  39.2 2.4 fusion.121
  42.9 3.1 %fusion.122 = f32[2,64,1024]{2,1,0:T(8,128)S(1)} fusion(s32[2,512]{1,0:T(2,128)S(1)} %copy-done.17, f32[2,2,64,1024]{3,2,1,0:T(8,128)S(1)} %fusion.121, f32[2,64,1024]{2,1,0:T(8,128)S(1)} %get-tuple-element.904, f32[2,64,1024]{2,1,0:T(8,128)S(1)} %get-tuple-element.927, f32[64,1024]{1,0:T(8,128)S(1)} %copy-done.12, ...), kind=kOutput, calls=%fused_computation.39.clone.1 | convolution fusion | flops 808452096 | bytes 2633984 | tf_op jit(solution)/shard_map/while/body/eval_jaxpr/szr,srx->szx/dot_general | solution.py:81
  47.8 1.3 collective-permute-start
  49.0 4.9 %collective-permute-start.1 = (f32[4,2,8,1024]{3,2,1,0:T(8,128)}, f32[4,2,8,1024]{3,2,1,0:T(8,128)S(1)}, u32[]{:S(2)}, u32[]{:S(2)}) collective-permute-start(f32[4,2,8,1024]{3,2,1,0:T(8,128)} %get-tuple-element.863), channel_id=1, source_target_pairs={{0,1},{1,2},{2,3},{4,5},{5,6},{6,7},{8,9},{9,10},{10,11},{12,13},{... | collective-permute-start | bytes 786440 | tf_op jit(solution)/shard_map/while/body/eval_jaxpr/ppermute | solution.py:19
  56.6 1.6 collective-permute-done.1
  58.5 2.6 fusion.117
  62.1 3.2 %fusion.118 = f32[2,72,1024]{2,1,0:T(8,128)S(1)} fusion(f32[2,2,72,1024]{3,2,1,0:T(8,128)S(1)} %fusion.117, f32[4,2,80,1024]{3,2,1,0:T(8,128)S(1)} %pad_maximum_fusion.23, s32[2,512]{1,0:T(2,128)S(1)} %copy-done.17, f32[72,1024]{1,0:T(8,128)S(1)} %bitcast.101, f32[72,1024]{1,0:T(8,128)S(1)} %bitcast.98, f32[2,512]{1,0:T(2,128)S(1)} %get-tuple-element.864, ...), kind=kOutput, calls=%fused_computation.109.clone.1 | convolution fusion | flops 909246464 | bytes 2961696 | tf_op jit(solution)/shard_map/while/body/eval_jaxpr/szr,srx->szx/dot_general | solution.py:81
  65.4 2.4 fusion.121
  69.1 3.1 %fusion.122 = f32[2,64,1024]{2,1,0:T(8,128)S(1)} fusion(s32[2,512]{1,0:T(2,128)S(1)} %copy-done.17, f32[2,2,64,1024]{3,2,1,0:T(8,128)S(1)} %fusion.121, f32[2,64,1024]{2,1,0:T(8,128)S(1)} %get-tuple-element.904, f32[2,64,1024]{2,1,0:T(8,128)S(1)} %get-tuple-element.927, f32[64,1024]{1,0:T(8,128)S(1)} %copy-done.12, ...), kind=kOutput, calls=%fused_computation.39.clone.1 | convolution fusion | flops 808452096 | bytes 2633984 | tf_op jit(solution)/shard_map/while/body/eval_jaxpr/szr,srx->szx/dot_general | solution.py:81
  73.9 1.3 collective-permute-start
  75.2 4.9 %collective-permute-start.1 = (f32[4,2,8,1024]{3,2,1,0:T(8,128)}, f32[4,2,8,1024]{3,2,1,0:T(8,128)S(1)}, u32[]{:S(2)}, u32[]{:S(2)}) collective-permute-start(f32[4,2,8,1024]{3,2,1,0:T(8,128)} %get-tuple-element.863), channel_id=1, source_target_pairs={{0,1},{1,2},{2,3},{4,5},{5,6},{6,7},{8,9},{9,10},{10,11},{12,13},{... | collective-permute-start | bytes 786440 | tf_op jit(solution)/shard_map/while/body/eval_jaxpr/ppermute | solution.py:19
  82.8 1.6 collective-permute-done.1
  84.7 2.6 fusion.117
  88.3 3.2 %fusion.118 = f32[2,72,1024]{2,1,0:T(8,128)S(1)} fusion(f32[2,2,72,1024]{3,2,1,0:T(8,128)S(1)} %fusion.117, f32[4,2,80,1024]{3,2,1,0:T(8,128)S(1)} %pad_maximum_fusion.23, s32[2,512]{1,0:T(2,128)S(1)} %copy-done.17, f32[72,1024]{1,0:T(8,128)S(1)} %bitcast.101, f32[72,1024]{1,0:T(8,128)S(1)} %bitcast.98, f32[2,512]{1,0:T(2,128)S(1)} %get-tuple-element.864, ...), kind=kOutput, calls=%fused_computation.109.clone.1 | convolution fusion | flops 909246464 | bytes 2961696 | tf_op jit(solution)/shard_map/while/body/eval_jaxpr/szr,srx->szx/dot_general | solution.py:81
  91.6 2.4 fusion.121
  95.2 3.1 %fusion.122 = f32[2,64,1024]{2,1,0:T(8,128)S(1)} fusion(s32[2,512]{1,0:T(2,128)S(1)} %copy-done.17, f32[2,2,64,1024]{3,2,1,0:T(8,128)S(1)} %fusion.121, f32[2,64,1024]{2,1,0:T(8,128)S(1)} %get-tuple-element.904, f32[2,64,1024]{2,1,0:T(8,128)S(1)} %get-tuple-element.927, f32[64,1024]{1,0:T(8,128)S(1)} %copy-done.12, ...), kind=kOutput, calls=%fused_computation.39.clone.1 | convolution fusion | flops 808452096 | bytes 2633984 | tf_op jit(solution)/shard_map/while/body/eval_jaxpr/szr,srx->szx/dot_general | solution.py:81
  100.1 1.3 collective-permute-start
  101.4 4.9 %collective-permute-start.1 = (f32[4,2,8,1024]{3,2,1,0:T(8,128)}, f32[4,2,8,1024]{3,2,1,0:T(8,128)S(1)}, u32[]{:S(2)}, u32[]{:S(2)}) collective-permute-start(f32[4,2,8,1024]{3,2,1,0:T(8,128)} %get-tuple-element.863), channel_id=1, source_target_pairs={{0,1},{1,2},{2,3},{4,5},{5,6},{6,7},{8,9},{9,10},{10,11},{12,13},{... | collective-permute-start | bytes 786440 | tf_op jit(solution)/shard_map/while/body/eval_jaxpr/ppermute | solution.py:19
  108.9 1.6 collective-permute-done.1
  110.8 2.6 fusion.117
  114.4 3.2 %fusion.118 = f32[2,72,1024]{2,1,0:T(8,128)S(1)} fusion(f32[2,2,72,1024]{3,2,1,0:T(8,128)S(1)} %fusion.117, f32[4,2,80,1024]{3,2,1,0:T(8,128)S(1)} %pad_maximum_fusion.23, s32[2,512]{1,0:T(2,128)S(1)} %copy-done.17, f32[72,1024]{1,0:T(8,128)S(1)} %bitcast.101, f32[72,1024]{1,0:T(8,128)S(1)} %bitcast.98, f32[2,512]{1,0:T(2,128)S(1)} %get-tuple-element.864, ...), kind=kOutput, calls=%fused_computation.109.clone.1 | convolution fusion | flops 909246464 | bytes 2961696 | tf_op jit(solution)/shard_map/while/body/eval_jaxpr/szr,srx->szx/dot_general | solution.py:81
  117.8 2.4 fusion.121
  121.4 3.1 %fusion.122 = f32[2,64,1024]{2,1,0:T(8,128)S(1)} fusion(s32[2,512]{1,0:T(2,128)S(1)} %copy-done.17, f32[2,2,64,1024]{3,2,1,0:T(8,128)S(1)} %fusion.121, f32[2,64,1024]{2,1,0:T(8,128)S(1)} %get-tuple-element.904, f32[2,64,1024]{2,1,0:T(8,128)S(1)} %get-tuple-element.927, f32[64,1024]{1,0:T(8,128)S(1)} %copy-done.12, ...), kind=kOutput, calls=%fused_computation.39.clone.1 | convolution fusion | flops 808452096 | bytes 2633984 | tf_op jit(solution)/shard_map/while/body/eval_jaxpr/szr,srx->szx/dot_general | solution.py:81
  126.3 1.3 collective-permute-start
  127.6 4.9 %collective-permute-start.1 = (f32[4,2,8,1024]{3,2,1,0:T(8,128)}, f32[4,2,8,1024]{3,2,1,0:T(8,128)S(1)}, u32[]{:S(2)}, u32[]{:S(2)}) collective-permute-start(f32[4,2,8,1024]{3,2,1,0:T(8,128)} %get-tuple-element.863), channel_id=1, source_target_pairs={{0,1},{1,2},{2,3},{4,5},{5,6},{6,7},{8,9},{9,10},{10,11},{12,13},{... | collective-permute-start | bytes 786440 | tf_op jit(solution)/shard_map/while/body/eval_jaxpr/ppermute | solution.py:19
  135.1 1.6 collective-permute-done.1
  137.0 2.6 fusion.117
  140.6 3.2 %fusion.118 = f32[2,72,1024]{2,1,0:T(8,128)S(1)} fusion(f32[2,2,72,1024]{3,2,1,0:T(8,128)S(1)} %fusion.117, f32[4,2,80,1024]{3,2,1,0:T(8,128)S(1)} %pad_maximum_fusion.23, s32[2,512]{1,0:T(2,128)S(1)} %copy-done.17, f32[72,1024]{1,0:T(8,128)S(1)} %bitcast.101, f32[72,1024]{1,0:T(8,128)S(1)} %bitcast.98, f32[2,512]{1,0:T(2,128)S(1)} %get-tuple-element.864, ...), kind=kOutput, calls=%fused_computation.109.clone.1 | convolution fusion | flops 909246464 | bytes 2961696 | tf_op jit(solution)/shard_map/while/body/eval_jaxpr/szr,srx->szx/dot_general | solution.py:81
  143.9 2.4 fusion.121
  147.6 3.1 %fusion.122 = f32[2,64,1024]{2,1,0:T(8,128)S(1)} fusion(s32[2,512]{1,0:T(2,128)S(1)} %copy-done.17, f32[2,2,64,1024]{3,2,1,0:T(8,128)S(1)} %fusion.121, f32[2,64,1024]{2,1,0:T(8,128)S(1)} %get-tuple-element.904, f32[2,64,1024]{2,1,0:T(8,128)S(1)} %get-tuple-element.927, f32[64,1024]{1,0:T(8,128)S(1)} %copy-done.12, ...), kind=kOutput, calls=%fused_computation.39.clone.1 | convolution fusion | flops 808452096 | bytes 2633984 | tf_op jit(solution)/shard_map/while/body/eval_jaxpr/szr,srx->szx/dot_general | solution.py:81
  152.4 1.3 collective-permute-start
  153.7 4.9 %collective-permute-start.1 = (f32[4,2,8,1024]{3,2,1,0:T(8,128)}, f32[4,2,8,1024]{3,2,1,0:T(8,128)S(1)}, u32[]{:S(2)}, u32[]{:S(2)}) collective-permute-start(f32[4,2,8,1024]{3,2,1,0:T(8,128)} %get-tuple-element.863), channel_id=1, source_target_pairs={{0,1},{1,2},{2,3},{4,5},{5,6},{6,7},{8,9},{9,10},{10,11},{12,13},{... | collective-permute-start | bytes 786440 | tf_op jit(solution)/shard_map/while/body/eval_jaxpr/ppermute | solution.py:19
  161.3 1.6 collective-permute-done.1
  163.2 2.6 fusion.117
  166.8 3.2 %fusion.118 = f32[2,72,1024]{2,1,0:T(8,128)S(1)} fusion(f32[2,2,72,1024]{3,2,1,0:T(8,128)S(1)} %fusion.117, f32[4,2,80,1024]{3,2,1,0:T(8,128)S(1)} %pad_maximum_fusion.23, s32[2,512]{1,0:T(2,128)S(1)} %copy-done.17, f32[72,1024]{1,0:T(8,128)S(1)} %bitcast.101, f32[72,1024]{1,0:T(8,128)S(1)} %bitcast.98, f32[2,512]{1,0:T(2,128)S(1)} %get-tuple-element.864, ...), kind=kOutput, calls=%fused_computation.109.clone.1 | convolution fusion | flops 909246464 | bytes 2961696 | tf_op jit(solution)/shard_map/while/body/eval_jaxpr/szr,srx->szx/dot_general | solution.py:81
  170.1 2.4 fusion.121
  173.8 3.1 %fusion.122 = f32[2,64,1024]{2,1,0:T(8,128)S(1)} fusion(s32[2,512]{1,0:T(2,128)S(1)} %copy-done.17, f32[2,2,64,1024]{3,2,1,0:T(8,128)S(1)} %fusion.121, f32[2,64,1024]{2,1,0:T(8,128)S(1)} %get-tuple-element.904, f32[2,64,1024]{2,1,0:T(8,128)S(1)} %get-tuple-element.927, f32[64,1024]{1,0:T(8,128)S(1)} %copy-done.12, ...), kind=kOutput, calls=%fused_computation.39.clone.1 | convolution fusion | flops 808452096 | bytes 2633984 | tf_op jit(solution)/shard_map/while/body/eval_jaxpr/szr,srx->szx/dot_general | solution.py:81
  178.6 1.3 collective-permute-start
  179.9 4.9 %collective-permute-start.1 = (f32[4,2,8,1024]{3,2,1,0:T(8,128)}, f32[4,2,8,1024]{3,2,1,0:T(8,128)S(1)}, u32[]{:S(2)}, u32[]{:S(2)}) collective-permute-start(f32[4,2,8,1024]{3,2,1,0:T(8,128)} %get-tuple-element.863), channel_id=1, source_target_pairs={{0,1},{1,2},{2,3},{4,5},{5,6},{6,7},{8,9},{9,10},{10,11},{12,13},{... | collective-permute-start | bytes 786440 | tf_op jit(solution)/shard_map/while/body/eval_jaxpr/ppermute | solution.py:19
  187.4 1.6 collective-permute-done.1
  189.4 2.6 fusion.117
  193.0 3.2 %fusion.118 = f32[2,72,1024]{2,1,0:T(8,128)S(1)} fusion(f32[2,2,72,1024]{3,2,1,0:T(8,128)S(1)} %fusion.117, f32[4,2,80,1024]{3,2,1,0:T(8,128)S(1)} %pad_maximum_fusion.23, s32[2,512]{1,0:T(2,128)S(1)} %copy-done.17, f32[72,1024]{1,0:T(8,128)S(1)} %bitcast.101, f32[72,1024]{1,0:T(8,128)S(1)} %bitcast.98, f32[2,512]{1,0:T(2,128)S(1)} %get-tuple-element.864, ...), kind=kOutput, calls=%fused_computation.109.clone.1 | convolution fusion | flops 909246464 | bytes 2961696 | tf_op jit(solution)/shard_map/while/body/eval_jaxpr/szr,srx->szx/dot_general | solution.py:81
  196.3 2.4 fusion.121
  199.9 3.1 %fusion.122 = f32[2,64,1024]{2,1,0:T(8,128)S(1)} fusion(s32[2,512]{1,0:T(2,128)S(1)} %copy-done.17, f32[2,2,64,1024]{3,2,1,0:T(8,128)S(1)} %fusion.121, f32[2,64,1024]{2,1,0:T(8,128)S(1)} %get-tuple-element.904, f32[2,64,1024]{2,1,0:T(8,128)S(1)} %get-tuple-element.927, f32[64,1024]{1,0:T(8,128)S(1)} %copy-done.12, ...), kind=kOutput, calls=%fused_computation.39.clone.1 | convolution fusion | flops 808452096 | bytes 2633984 | tf_op jit(solution)/shard_map/while/body/eval_jaxpr/szr,srx->szx/dot_general | solution.py:81
  204.8 1.3 collective-permute-start
  206.1 4.9 %collective-permute-start.1 = (f32[4,2,8,1024]{3,2,1,0:T(8,128)}, f32[4,2,8,1024]{3,2,1,0:T(8,128)S(1)}, u32[]{:S(2)}, u32[]{:S(2)}) collective-permute-start(f32[4,2,8,1024]{3,2,1,0:T(8,128)} %get-tuple-element.863), channel_id=1, source_target_pairs={{0,1},{1,2},{2,3},{4,5},{5,6},{6,7},{8,9},{9,10},{10,11},{12,13},{... | collective-permute-start | bytes 786440 | tf_op jit(solution)/shard_map/while/body/eval_jaxpr/ppermute | solution.py:19
  213.6 1.6 collective-permute-done.1
  215.5 2.6 fusion.117
  219.1 3.2 %fusion.118 = f32[2,72,1024]{2,1,0:T(8,128)S(1)} fusion(f32[2,2,72,1024]{3,2,1,0:T(8,128)S(1)} %fusion.117, f32[4,2,80,1024]{3,2,1,0:T(8,128)S(1)} %pad_maximum_fusion.23, s32[2,512]{1,0:T(2,128)S(1)} %copy-done.17, f32[72,1024]{1,0:T(8,128)S(1)} %bitcast.101, f32[72,1024]{1,0:T(8,128)S(1)} %bitcast.98, f32[2,512]{1,0:T(2,128)S(1)} %get-tuple-element.864, ...), kind=kOutput, calls=%fused_computation.109.clone.1 | convolution fusion | flops 909246464 | bytes 2961696 | tf_op jit(solution)/shard_map/while/body/eval_jaxpr/szr,srx->szx/dot_general | solution.py:81
  222.4 2.4 fusion.121
  226.1 3.1 %fusion.122 = f32[2,64,1024]{2,1,0:T(8,128)S(1)} fusion(s32[2,512]{1,0:T(2,128)S(1)} %copy-done.17, f32[2,2,64,1024]{3,2,1,0:T(8,128)S(1)} %fusion.121, f32[2,64,1024]{2,1,0:T(8,128)S(1)} %get-tuple-element.904, f32[2,64,1024]{2,1,0:T(8,128)S(1)} %get-tuple-element.927, f32[64,1024]{1,0:T(8,128)S(1)} %copy-done.12, ...), kind=kOutput, calls=%fused_computation.39.clone.1 | convolution fusion | flops 808452096 | bytes 2633984 | tf_op jit(solution)/shard_map/while/body/eval_jaxpr/szr,srx->szx/dot_general | solution.py:81
  230.2 35.4 %all-reduce.4.cloned.1.call-done = f32[64,1024]{1,0:T(8,128)} async-done(((f32[64,1024]{1,0:T(8,128)}), f32[64,1024]{1,0:T(8,128)}) %all-reduce.4.cloned.1.call-update) | async-done | bytes 262160 | tf_op jit(solution)/shard_map/psum | solution.py:143
  265.6 1.7 broadcast_multiply_fusion
  (370 shorter events, 57.0 us)
Async XLA Ops:
  7.2 258.4 %all-reduce.4.cloned.1.call-start = ((), (), s32[]{:S(2)}) async-start(), calls=%async_computation | async-start | bytes 524288 | tf_op jit(solution)/shard_map/psum | solution.py:143
  7.2 1.7 copy-start.7
  7.2 8.2 %copy-start.13 = (f32[2,16,512]{2,1,0:T(8,128)S(1)}, f32[2,16,512]{2,1,0:T(8,128)}, u32[]{:S(2)}) copy-start(f32[2,16,512]{2,1,0:T(8,128)} %param.21) | copy-start | bytes 196612
  8.2 12.9 %copy-start.6 = (f32[2,64,1024]{2,1,0:T(8,128)S(1)}, f32[2,64,1024]{2,1,0:T(8,128)}, u32[]{:S(2)}) copy-start(f32[2,64,1024]{2,1,0:T(8,128)} %param.19) | copy-start | bytes 1572868
  8.9 12.1 %copy-start = (f32[256]{0:T(256)S(1)}, f32[256]{0:T(256)}, u32[]{:S(2)}) copy-start(f32[256]{0:T(256)} %param.22) | copy-start | bytes 3076
  8.9 12.1 %copy-start.1 = (f32[2,64,1024]{2,1,0:T(8,128)S(1)}, f32[2,64,1024]{2,1,0:T(8,128)}, u32[]{:S(2)}) copy-start(f32[2,64,1024]{2,1,0:T(8,128)} %param.17) | copy-start | bytes 1572868
  8.9 12.1 %copy-start.3 = (f32[2,64,1024]{2,1,0:T(8,128)S(1)}, f32[2,64,1024]{2,1,0:T(8,128)}, u32[]{:S(2)}) copy-start(f32[2,64,1024]{2,1,0:T(8,128)} %param.18) | copy-start | bytes 1572868
  8.9 12.1 %copy-start.5 = (f32[2,64,1024]{2,1,0:T(8,128)S(1)}, f32[2,64,1024]{2,1,0:T(8,128)}, u32[]{:S(2)}) copy-start(f32[2,64,1024]{2,1,0:T(8,128)} %param.20) | copy-start | bytes 1572868
  8.9 12.1 %copy-start.14 = (s32[2]{0:T(128)S(1)}, s32[2]{0:T(128)}, u32[]{:S(2)}) copy-start(s32[2]{0:T(128)} %param.27) | copy-start | bytes 28
  8.9 12.1 %copy-start.15 = (s32[2]{0:T(128)S(1)}, s32[2]{0:T(128)}, u32[]{:S(2)}) copy-start(s32[2]{0:T(128)} %param.24) | copy-start | bytes 28
  8.9 12.1 %copy-start.16 = (s32[2,512]{1,0:T(2,128)S(1)}, s32[2,512]{1,0:T(2,128)}, u32[]{:S(2)}) copy-start(s32[2,512]{1,0:T(2,128)} %param.25) | copy-start | bytes 12292
  9.0 12.1 %copy-start.18 = (s32[2]{0:T(128)S(1)}, s32[2]{0:T(128)}, u32[]{:S(2)}) copy-start(s32[2]{0:T(128)} %param.23) | copy-start | bytes 28
  9.0 7.0 %collective-permute-start.2 = (f32[2,8,1024]{2,1,0:T(8,128)S(1)}, f32[2,8,1024]{2,1,0:T(8,128)S(1)}, u32[]{:S(2)}, u32[]{:S(2)}) collective-permute-start(f32[2,8,1024]{2,1,0:T(8,128)S(1)} %get-tuple-element.729), channel_id=1, source_target_pairs={{0,1},{1,2},{2,3},{4,5},{5,6},{6,7},{8,9},{9,10},{10,11},{12,13},{... | collective-permute-start | bytes 196616 | tf_op jit(solution)/shard_map/ppermute | solution.py:19
  14.1 6.2 %collective-permute-start.3 = (f32[2,8,1024]{2,1,0:T(8,128)S(1)}, f32[2,8,1024]{2,1,0:T(8,128)S(1)}, u32[]{:S(2)}, u32[]{:S(2)}) collective-permute-start(f32[2,8,1024]{2,1,0:T(8,128)S(1)} %get-tuple-element.730), channel_id=1, source_target_pairs={{1,0},{2,1},{3,2},{5,4},{6,5},{7,6},{9,8},{10,9},{11,10},{13,12},{... | collective-permute-start | bytes 196616 | tf_op jit(solution)/shard_map/ppermute | solution.py:21
  21.9 8.7 %collective-permute-start = (f32[4,2,8,1024]{3,2,1,0:T(8,128)}, f32[4,2,8,1024]{3,2,1,0:T(8,128)S(1)}, u32[]{:S(2)}, u32[]{:S(2)}) collective-permute-start(f32[4,2,8,1024]{3,2,1,0:T(8,128)} %get-tuple-element.862), channel_id=1, source_target_pairs={{1,0},{2,1},{3,2},{5,4},{6,5},{7,6},{9,8},{10,9},{11,10},{13,12},{... | collective-permute-start | bytes 786440 | tf_op jit(solution)/shard_map/while/body/eval_jaxpr/ppermute | solution.py:21
  23.2 8.7 %collective-permute-start.1 = (f32[4,2,8,1024]{3,2,1,0:T(8,128)}, f32[4,2,8,1024]{3,2,1,0:T(8,128)S(1)}, u32[]{:S(2)}, u32[]{:S(2)}) collective-permute-start(f32[4,2,8,1024]{3,2,1,0:T(8,128)} %get-tuple-element.863), channel_id=1, source_target_pairs={{0,1},{1,2},{2,3},{4,5},{5,6},{6,7},{8,9},{9,10},{10,11},{12,13},{... | collective-permute-start | bytes 786440 | tf_op jit(solution)/shard_map/while/body/eval_jaxpr/ppermute | solution.py:19
  35.0 1.0 copy-start.10
  35.0 1.0 copy-start.17
  42.9 3.1 %copy-start.8 = (f32[64,1024]{1,0:T(8,128)S(1)}, f32[64,1024]{1,0:T(8,128)}, u32[]{:S(2)}) copy-start(f32[64,1024]{1,0:T(8,128)} %get-tuple-element.905) | copy-start | bytes 786436 | tf_op jit(solution)/shard_map/while
  42.9 4.0 %copy-start.19 = (s32[2]{0:T(128)S(1)}, s32[2]{0:T(128)}, u32[]{:S(2)}) copy-start(s32[2]{0:T(128)} %get-tuple-element.982) | copy-start | bytes 28 | tf_op jit(solution)/shard_map/while
  47.8 8.8 %collective-permute-start = (f32[4,2,8,1024]{3,2,1,0:T(8,128)}, f32[4,2,8,1024]{3,2,1,0:T(8,128)S(1)}, u32[]{:S(2)}, u32[]{:S(2)}) collective-permute-start(f32[4,2,8,1024]{3,2,1,0:T(8,128)} %get-tuple-element.862), channel_id=1, source_target_pairs={{1,0},{2,1},{3,2},{5,4},{6,5},{7,6},{9,8},{10,9},{11,10},{13,12},{... | collective-permute-start | bytes 786440 | tf_op jit(solution)/shard_map/while/body/eval_jaxpr/ppermute | solution.py:21
  49.0 9.1 %collective-permute-start.1 = (f32[4,2,8,1024]{3,2,1,0:T(8,128)}, f32[4,2,8,1024]{3,2,1,0:T(8,128)S(1)}, u32[]{:S(2)}, u32[]{:S(2)}) collective-permute-start(f32[4,2,8,1024]{3,2,1,0:T(8,128)} %get-tuple-element.863), channel_id=1, source_target_pairs={{0,1},{1,2},{2,3},{4,5},{5,6},{6,7},{8,9},{9,10},{10,11},{12,13},{... | collective-permute-start | bytes 786440 | tf_op jit(solution)/shard_map/while/body/eval_jaxpr/ppermute | solution.py:19
  61.1 1.0 copy-start.10
  61.1 1.0 copy-start.17
  69.1 3.1 %copy-start.8 = (f32[64,1024]{1,0:T(8,128)S(1)}, f32[64,1024]{1,0:T(8,128)}, u32[]{:S(2)}) copy-start(f32[64,1024]{1,0:T(8,128)} %get-tuple-element.905) | copy-start | bytes 786436 | tf_op jit(solution)/shard_map/while
  69.1 4.0 %copy-start.19 = (s32[2]{0:T(128)S(1)}, s32[2]{0:T(128)}, u32[]{:S(2)}) copy-start(s32[2]{0:T(128)} %get-tuple-element.982) | copy-start | bytes 28 | tf_op jit(solution)/shard_map/while
  73.9 8.8 %collective-permute-start = (f32[4,2,8,1024]{3,2,1,0:T(8,128)}, f32[4,2,8,1024]{3,2,1,0:T(8,128)S(1)}, u32[]{:S(2)}, u32[]{:S(2)}) collective-permute-start(f32[4,2,8,1024]{3,2,1,0:T(8,128)} %get-tuple-element.862), channel_id=1, source_target_pairs={{1,0},{2,1},{3,2},{5,4},{6,5},{7,6},{9,8},{10,9},{11,10},{13,12},{... | collective-permute-start | bytes 786440 | tf_op jit(solution)/shard_map/while/body/eval_jaxpr/ppermute | solution.py:21
  75.2 9.1 %collective-permute-start.1 = (f32[4,2,8,1024]{3,2,1,0:T(8,128)}, f32[4,2,8,1024]{3,2,1,0:T(8,128)S(1)}, u32[]{:S(2)}, u32[]{:S(2)}) collective-permute-start(f32[4,2,8,1024]{3,2,1,0:T(8,128)} %get-tuple-element.863), channel_id=1, source_target_pairs={{0,1},{1,2},{2,3},{4,5},{5,6},{6,7},{8,9},{9,10},{10,11},{12,13},{... | collective-permute-start | bytes 786440 | tf_op jit(solution)/shard_map/while/body/eval_jaxpr/ppermute | solution.py:19
  87.3 1.0 copy-start.10
  87.3 1.0 copy-start.17
  95.2 3.1 %copy-start.8 = (f32[64,1024]{1,0:T(8,128)S(1)}, f32[64,1024]{1,0:T(8,128)}, u32[]{:S(2)}) copy-start(f32[64,1024]{1,0:T(8,128)} %get-tuple-element.905) | copy-start | bytes 786436 | tf_op jit(solution)/shard_map/while
  95.2 4.0 %copy-start.19 = (s32[2]{0:T(128)S(1)}, s32[2]{0:T(128)}, u32[]{:S(2)}) copy-start(s32[2]{0:T(128)} %get-tuple-element.982) | copy-start | bytes 28 | tf_op jit(solution)/shard_map/while
  100.1 8.8 %collective-permute-start = (f32[4,2,8,1024]{3,2,1,0:T(8,128)}, f32[4,2,8,1024]{3,2,1,0:T(8,128)S(1)}, u32[]{:S(2)}, u32[]{:S(2)}) collective-permute-start(f32[4,2,8,1024]{3,2,1,0:T(8,128)} %get-tuple-element.862), channel_id=1, source_target_pairs={{1,0},{2,1},{3,2},{5,4},{6,5},{7,6},{9,8},{10,9},{11,10},{13,12},{... | collective-permute-start | bytes 786440 | tf_op jit(solution)/shard_map/while/body/eval_jaxpr/ppermute | solution.py:21
  101.4 9.1 %collective-permute-start.1 = (f32[4,2,8,1024]{3,2,1,0:T(8,128)}, f32[4,2,8,1024]{3,2,1,0:T(8,128)S(1)}, u32[]{:S(2)}, u32[]{:S(2)}) collective-permute-start(f32[4,2,8,1024]{3,2,1,0:T(8,128)} %get-tuple-element.863), channel_id=1, source_target_pairs={{0,1},{1,2},{2,3},{4,5},{5,6},{6,7},{8,9},{9,10},{10,11},{12,13},{... | collective-permute-start | bytes 786440 | tf_op jit(solution)/shard_map/while/body/eval_jaxpr/ppermute | solution.py:19
  113.5 1.0 copy-start.10
  113.5 1.0 copy-start.17
  121.4 3.1 %copy-start.8 = (f32[64,1024]{1,0:T(8,128)S(1)}, f32[64,1024]{1,0:T(8,128)}, u32[]{:S(2)}) copy-start(f32[64,1024]{1,0:T(8,128)} %get-tuple-element.905) | copy-start | bytes 786436 | tf_op jit(solution)/shard_map/while
  121.4 4.0 %copy-start.19 = (s32[2]{0:T(128)S(1)}, s32[2]{0:T(128)}, u32[]{:S(2)}) copy-start(s32[2]{0:T(128)} %get-tuple-element.982) | copy-start | bytes 28 | tf_op jit(solution)/shard_map/while
  126.3 8.8 %collective-permute-start = (f32[4,2,8,1024]{3,2,1,0:T(8,128)}, f32[4,2,8,1024]{3,2,1,0:T(8,128)S(1)}, u32[]{:S(2)}, u32[]{:S(2)}) collective-permute-start(f32[4,2,8,1024]{3,2,1,0:T(8,128)} %get-tuple-element.862), channel_id=1, source_target_pairs={{1,0},{2,1},{3,2},{5,4},{6,5},{7,6},{9,8},{10,9},{11,10},{13,12},{... | collective-permute-start | bytes 786440 | tf_op jit(solution)/shard_map/while/body/eval_jaxpr/ppermute | solution.py:21
  127.6 9.1 %collective-permute-start.1 = (f32[4,2,8,1024]{3,2,1,0:T(8,128)}, f32[4,2,8,1024]{3,2,1,0:T(8,128)S(1)}, u32[]{:S(2)}, u32[]{:S(2)}) collective-permute-start(f32[4,2,8,1024]{3,2,1,0:T(8,128)} %get-tuple-element.863), channel_id=1, source_target_pairs={{0,1},{1,2},{2,3},{4,5},{5,6},{6,7},{8,9},{9,10},{10,11},{12,13},{... | collective-permute-start | bytes 786440 | tf_op jit(solution)/shard_map/while/body/eval_jaxpr/ppermute | solution.py:19
  139.6 1.0 copy-start.10
  139.7 1.0 copy-start.17
  147.6 3.1 %copy-start.8 = (f32[64,1024]{1,0:T(8,128)S(1)}, f32[64,1024]{1,0:T(8,128)}, u32[]{:S(2)}) copy-start(f32[64,1024]{1,0:T(8,128)} %get-tuple-element.905) | copy-start | bytes 786436 | tf_op jit(solution)/shard_map/while
  147.6 4.0 %copy-start.19 = (s32[2]{0:T(128)S(1)}, s32[2]{0:T(128)}, u32[]{:S(2)}) copy-start(s32[2]{0:T(128)} %get-tuple-element.982) | copy-start | bytes 28 | tf_op jit(solution)/shard_map/while
  152.4 8.8 %collective-permute-start = (f32[4,2,8,1024]{3,2,1,0:T(8,128)}, f32[4,2,8,1024]{3,2,1,0:T(8,128)S(1)}, u32[]{:S(2)}, u32[]{:S(2)}) collective-permute-start(f32[4,2,8,1024]{3,2,1,0:T(8,128)} %get-tuple-element.862), channel_id=1, source_target_pairs={{1,0},{2,1},{3,2},{5,4},{6,5},{7,6},{9,8},{10,9},{11,10},{13,12},{... | collective-permute-start | bytes 786440 | tf_op jit(solution)/shard_map/while/body/eval_jaxpr/ppermute | solution.py:21
  153.7 9.1 %collective-permute-start.1 = (f32[4,2,8,1024]{3,2,1,0:T(8,128)}, f32[4,2,8,1024]{3,2,1,0:T(8,128)S(1)}, u32[]{:S(2)}, u32[]{:S(2)}) collective-permute-start(f32[4,2,8,1024]{3,2,1,0:T(8,128)} %get-tuple-element.863), channel_id=1, source_target_pairs={{0,1},{1,2},{2,3},{4,5},{5,6},{6,7},{8,9},{9,10},{10,11},{12,13},{... | collective-permute-start | bytes 786440 | tf_op jit(solution)/shard_map/while/body/eval_jaxpr/ppermute | solution.py:19
  165.8 1.0 copy-start.10
  165.8 1.0 copy-start.17
  173.8 3.1 %copy-start.8 = (f32[64,1024]{1,0:T(8,128)S(1)}, f32[64,1024]{1,0:T(8,128)}, u32[]{:S(2)}) copy-start(f32[64,1024]{1,0:T(8,128)} %get-tuple-element.905) | copy-start | bytes 786436 | tf_op jit(solution)/shard_map/while
  173.8 4.0 %copy-start.19 = (s32[2]{0:T(128)S(1)}, s32[2]{0:T(128)}, u32[]{:S(2)}) copy-start(s32[2]{0:T(128)} %get-tuple-element.982) | copy-start | bytes 28 | tf_op jit(solution)/shard_map/while
  178.6 8.8 %collective-permute-start = (f32[4,2,8,1024]{3,2,1,0:T(8,128)}, f32[4,2,8,1024]{3,2,1,0:T(8,128)S(1)}, u32[]{:S(2)}, u32[]{:S(2)}) collective-permute-start(f32[4,2,8,1024]{3,2,1,0:T(8,128)} %get-tuple-element.862), channel_id=1, source_target_pairs={{1,0},{2,1},{3,2},{5,4},{6,5},{7,6},{9,8},{10,9},{11,10},{13,12},{... | collective-permute-start | bytes 786440 | tf_op jit(solution)/shard_map/while/body/eval_jaxpr/ppermute | solution.py:21
  179.9 9.1 %collective-permute-start.1 = (f32[4,2,8,1024]{3,2,1,0:T(8,128)}, f32[4,2,8,1024]{3,2,1,0:T(8,128)S(1)}, u32[]{:S(2)}, u32[]{:S(2)}) collective-permute-start(f32[4,2,8,1024]{3,2,1,0:T(8,128)} %get-tuple-element.863), channel_id=1, source_target_pairs={{0,1},{1,2},{2,3},{4,5},{5,6},{6,7},{8,9},{9,10},{10,11},{12,13},{... | collective-permute-start | bytes 786440 | tf_op jit(solution)/shard_map/while/body/eval_jaxpr/ppermute | solution.py:19
  192.0 1.0 copy-start.10
  192.0 1.0 copy-start.17
  199.9 3.1 %copy-start.8 = (f32[64,1024]{1,0:T(8,128)S(1)}, f32[64,1024]{1,0:T(8,128)}, u32[]{:S(2)}) copy-start(f32[64,1024]{1,0:T(8,128)} %get-tuple-element.905) | copy-start | bytes 786436 | tf_op jit(solution)/shard_map/while
  199.9 4.0 %copy-start.19 = (s32[2]{0:T(128)S(1)}, s32[2]{0:T(128)}, u32[]{:S(2)}) copy-start(s32[2]{0:T(128)} %get-tuple-element.982) | copy-start | bytes 28 | tf_op jit(solution)/shard_map/while
  204.8 8.8 %collective-permute-start = (f32[4,2,8,1024]{3,2,1,0:T(8,128)}, f32[4,2,8,1024]{3,2,1,0:T(8,128)S(1)}, u32[]{:S(2)}, u32[]{:S(2)}) collective-permute-start(f32[4,2,8,1024]{3,2,1,0:T(8,128)} %get-tuple-element.862), channel_id=1, source_target_pairs={{1,0},{2,1},{3,2},{5,4},{6,5},{7,6},{9,8},{10,9},{11,10},{13,12},{... | collective-permute-start | bytes 786440 | tf_op jit(solution)/shard_map/while/body/eval_jaxpr/ppermute | solution.py:21
  206.1 9.1 %collective-permute-start.1 = (f32[4,2,8,1024]{3,2,1,0:T(8,128)}, f32[4,2,8,1024]{3,2,1,0:T(8,128)S(1)}, u32[]{:S(2)}, u32[]{:S(2)}) collective-permute-start(f32[4,2,8,1024]{3,2,1,0:T(8,128)} %get-tuple-element.863), channel_id=1, source_target_pairs={{0,1},{1,2},{2,3},{4,5},{5,6},{6,7},{8,9},{9,10},{10,11},{12,13},{... | collective-permute-start | bytes 786440 | tf_op jit(solution)/shard_map/while/body/eval_jaxpr/ppermute | solution.py:19
  218.2 1.0 copy-start.10
  218.2 1.0 copy-start.17
  226.1 3.1 %copy-start.8 = (f32[64,1024]{1,0:T(8,128)S(1)}, f32[64,1024]{1,0:T(8,128)}, u32[]{:S(2)}) copy-start(f32[64,1024]{1,0:T(8,128)} %get-tuple-element.905) | copy-start | bytes 786436 | tf_op jit(solution)/shard_map/while
  226.1 4.0 %copy-start.19 = (s32[2]{0:T(128)S(1)}, s32[2]{0:T(128)}, u32[]{:S(2)}) copy-start(s32[2]{0:T(128)} %get-tuple-element.982) | copy-start | bytes 28 | tf_op jit(solution)/shard_map/while
  230.1 37.1 %copy-start.2 = (f32[2,64,1024]{2,1,0:T(8,128)}, f32[2,64,1024]{2,1,0:T(8,128)S(1)}, u32[]{:S(2)}) copy-start(f32[2,64,1024]{2,1,0:T(8,128)S(1)} %get-tuple-element.960) | copy-start | bytes 1572868
  230.1 37.1 %copy-start.4 = (f32[2,64,1024]{2,1,0:T(8,128)}, f32[2,64,1024]{2,1,0:T(8,128)S(1)}, u32[]{:S(2)}) copy-start(f32[2,64,1024]{2,1,0:T(8,128)S(1)} %get-tuple-element.962) | copy-start | bytes 1572868
  (49 other events, 38.4 us)
Sparse Core Ops, SparseCore 0:
  230.3 35.2 all-reduce.3
where the time goes:
time: 275 us; the launch traced here: 274 us
  other arithmetic  63.9 us (23%)
  waiting for transfers between devices  56.8 us (21%)
  starting transfers between devices  55.7 us (20%)
  matrix products  50.3 us (18%)
  local copies, waits for them, and re-layouts  31.5 us (11%)
  between operations  14.2 us (5%)
    dot_general x16, matrix products, advance(): jnp.einsum('szr,srx->szx', depth_table, lateral_table, precision=lax.Prec...  50.3 us
    ppermute x9, starting transfers between devices, extended_2(): lax.ppermute(tail, axis, [(i, (i + 1) % count) for i in range(ends)])  44.1 us
    add x16, other arithmetic, laplace(): result + stencil_coeffs[offset] * (extended[..., 4 + offset:4 + offset +...  39.8 us
    psum x1, waiting for transfers between devices, local(): image_total = lax.psum(carry[4], 'shot')  35.4 us
    while x160, local copies, waits for them, and re-layouts  18.2 us
    ppermute x9, waiting for transfers between devices, extended_2(): lax.ppermute(tail, axis, [(i, (i + 1) % count) for i in range(ends)])  12.8 us
    ppermute x9, starting transfers between devices, extended_2(): lax.ppermute(head, axis, [((i + 1) % count, i) for i in range(ends)])  11.5 us
    gather x16, local copies, waits for them, and re-layouts, advance(): pulse = wavelet[checkpoint_step + STEPS - 1 - step_index]  10.2 us
  transfers between devices with their start and end apart: 19, of which 19 were waited for; matrix products, arithmetic and copies ran while one was open for 5% of the time, Pallas kernels for 0%

commit v1 on v0

--- a/solution.py
+++ b/solution.py
@@ -140,7 +140,7 @@
     )
     source_final = carry[1]
     receiver_final = carry[3]
-    image_total = lax.psum(carry[4], "shot")
+    image_total = jnp.sum(lax.all_gather(carry[4], "shot"), axis=0)
     shots_all = lax.axis_size("shot") * source_now.shape[0]
     image = image_total / math.sqrt(STEPS * shots_all)
     return (image, source_final, receiver_final)

time: 275 us -> 260 us (0.945)
  waiting for transfers between devices: 56.8 us -> 41.2 us
    psum x1 -> x0, waiting for transfers between devices: 35.4 us -> none  [local(): image_total = lax.psum(carry[4], 'shot')]
    all_gather x0 -> x1, waiting for transfers between devices: none -> 19.8 us  [local(): image_total = jnp.sum(lax.all_gather(carry[4], 'shot'), axis=0)]
where the time goes in v1:
time: 260 us; the launch traced here: 259 us
  other arithmetic  64.2 us (25%)
  starting transfers between devices  55.7 us (21%)
  matrix products  50.3 us (19%)
  waiting for transfers between devices  41.2 us (16%)
  local copies, waits for them, and re-layouts  31.5 us (12%)
  between operations  14.2 us (5%)
    dot_general x16, matrix products, advance(): jnp.einsum('szr,srx->szx', depth_table, lateral_table, precision=lax.Prec...  50.3 us
    ppermute x9, starting transfers between devices, extended_2(): lax.ppermute(tail, axis, [(i, (i + 1) % count) for i in range(ends)])  44.1 us
    add x16, other arithmetic, laplace(): result + stencil_coeffs[offset] * (extended[..., 4 + offset:4 + offset +...  39.8 us
    all_gather x1, waiting for transfers between devices, local(): image_total = jnp.sum(lax.all_gather(carry[4], 'shot'), axis=0)  19.8 us
    while x160, local copies, waits for them, and re-layouts  18.2 us
    ppermute x9, waiting for transfers between devices, extended_2(): lax.ppermute(tail, axis, [(i, (i + 1) % count) for i in range(ends)])  12.8 us
    ppermute x9, starting transfers between devices, extended_2(): lax.ppermute(head, axis, [((i + 1) % count, i) for i in range(ends)])  11.5 us
    gather x16, local copies, waits for them, and re-layouts, advance(): pulse = wavelet[checkpoint_step + STEPS - 1 - step_index]  10.2 us
  transfers between devices with their start and end apart: 19, of which 19 were waited for; matrix products, arithmetic and copies ran while one was open for 5% of the time, Pallas kernels for 0%

profile of v1, /device:TPU:0, one launch (start us, length us, event | category | flops | bytes accessed | tf_op | source)
XLA Modules:
  0.0 258.9 jit_solution(11794666047563097001)
XLA Ops:
  7.2 0.9 copy-done.11
  9.0 5.1 %collective-permute-start.2 = (f32[2,8,1024]{2,1,0:T(8,128)S(1)}, f32[2,8,1024]{2,1,0:T(8,128)S(1)}, u32[]{:S(2)}, u32[]{:S(2)}) collective-permute-start(f32[2,8,1024]{2,1,0:T(8,128)S(1)} %get-tuple-element.729), channel_id=1, source_target_pairs={{0,1},{1,2},{2,3},{4,5},{5,6},{6,7},{8,9},{9,10},{10,11},{12,13},{... | collective-permute-start | bytes 196616 | tf_op jit(solution)/shard_map/ppermute | solution.py:19
  14.1 1.3 collective-permute-start.3
  16.0 4.3 %collective-permute-done.3 = f32[2,8,1024]{2,1,0:T(8,128)S(1)} collective-permute-done((f32[2,8,1024]{2,1,0:T(8,128)S(1)}, f32[2,8,1024]{2,1,0:T(8,128)S(1)}, u32[]{:S(2)}, u32[]{:S(2)}) %collective-permute-start.3) | collective-permute-done | bytes 65568 | tf_op jit(solution)/shard_map/ppermute | solution.py:21
  21.1 209.0 %while.26 = (s32[]{:T(128)}, f32[2,64,1024]{2,1,0:T(8,128)S(1)}, f32[2,64,1024]{2,1,0:T(8,128)S(1)}, f32[2,64,1024]{2,1,0:T(8,128)S(1)}, f32[2,64,1024]{2,1,0:T(...) while((s32[]{:T(128)}, f32[2,64,1024]{2,1,0:T(8,128)S(1)}, ...), condition=%wide.region_3.4_spmd.clone, body=%wide.region_0.3_spmd.clone.sunk | while | flops 1741394304 | bytes 51560036 | solution.py:135
  21.1 0.8 pad_maximum_fusion.22
  21.9 1.3 collective-permute-start
  23.2 4.6 %collective-permute-start.1 = (f32[4,2,8,1024]{3,2,1,0:T(8,128)}, f32[4,2,8,1024]{3,2,1,0:T(8,128)S(1)}, u32[]{:S(2)}, u32[]{:S(2)}) collective-permute-start(f32[4,2,8,1024]{3,2,1,0:T(8,128)} %get-tuple-element.863), channel_id=1, source_target_pairs={{0,1},{1,2},{2,3},{4,5},{5,6},{6,7},{8,9},{9,10},{10,11},{12,13},{... | collective-permute-start | bytes 786440 | tf_op jit(solution)/shard_map/while/body/eval_jaxpr/ppermute | solution.py:19
  30.7 1.3 collective-permute-done.1
  32.3 2.6 %fusion.117 = f32[2,2,72,1024]{3,2,1,0:T(8,128)S(1)} fusion(f32[2,2,72,1024]{3,2,1,0:T(8,128)S(1)} %slice.1057, f32[4,2,8,1024]{3,2,1,0:T(8,128)S(1)} %collective-permute-done.1, f32[1,2,64,1024]{3,2,1,0:T(8,128)S(1)} %bitcast.94, f32[1,2,64,1024]{3,2,1,0:T(8,128)S(1)} %bitcast.85, f32[1,2,64,1024]{3,2,1,0:T(8,128)S(1)} %bitcast.91, ...), kind=kLoop, calls=%fused_computation.46.clone.1 | loop fusion | flops 8552448 | bytes 12058624 | tf_op jit(solution)/shard_map/while/body/eval_jaxpr/add | solution.py:36
  35.9 3.2 %fusion.118 = f32[2,72,1024]{2,1,0:T(8,128)S(1)} fusion(f32[2,2,72,1024]{3,2,1,0:T(8,128)S(1)} %fusion.117, f32[4,2,80,1024]{3,2,1,0:T(8,128)S(1)} %pad_maximum_fusion.23, s32[2,512]{1,0:T(2,128)S(1)} %copy-done.17, f32[72,1024]{1,0:T(8,128)S(1)} %bitcast.103, f32[72,1024]{1,0:T(8,128)S(1)} %bitcast.99, f32[2,512]{1,0:T(2,128)S(1)} %get-tuple-element.864, ...), kind=kOutput, calls=%fused_computation.109.clone.1 | convolution fusion | flops 909246464 | bytes 2961696 | tf_op jit(solution)/shard_map/while/body/eval_jaxpr/szr,srx->szx/dot_general | solution.py:81
  39.2 2.4 fusion.121
  42.9 3.1 %fusion.122 = f32[2,64,1024]{2,1,0:T(8,128)S(1)} fusion(s32[2,512]{1,0:T(2,128)S(1)} %copy-done.17, f32[2,2,64,1024]{3,2,1,0:T(8,128)S(1)} %fusion.121, f32[2,64,1024]{2,1,0:T(8,128)S(1)} %get-tuple-element.904, f32[2,64,1024]{2,1,0:T(8,128)S(1)} %get-tuple-element.927, f32[64,1024]{1,0:T(8,128)S(1)} %copy-done.12, ...), kind=kOutput, calls=%fused_computation.39.clone.1 | convolution fusion | flops 808452096 | bytes 2633984 | tf_op jit(solution)/shard_map/while/body/eval_jaxpr/szr,srx->szx/dot_general | solution.py:81
  47.8 1.3 collective-permute-start
  49.0 4.9 %collective-permute-start.1 = (f32[4,2,8,1024]{3,2,1,0:T(8,128)}, f32[4,2,8,1024]{3,2,1,0:T(8,128)S(1)}, u32[]{:S(2)}, u32[]{:S(2)}) collective-permute-start(f32[4,2,8,1024]{3,2,1,0:T(8,128)} %get-tuple-element.863), channel_id=1, source_target_pairs={{0,1},{1,2},{2,3},{4,5},{5,6},{6,7},{8,9},{9,10},{10,11},{12,13},{... | collective-permute-start | bytes 786440 | tf_op jit(solution)/shard_map/while/body/eval_jaxpr/ppermute | solution.py:19
  56.6 1.6 collective-permute-done.1
  58.5 2.6 %fusion.117 = f32[2,2,72,1024]{3,2,1,0:T(8,128)S(1)} fusion(f32[2,2,72,1024]{3,2,1,0:T(8,128)S(1)} %slice.1057, f32[4,2,8,1024]{3,2,1,0:T(8,128)S(1)} %collective-permute-done.1, f32[1,2,64,1024]{3,2,1,0:T(8,128)S(1)} %bitcast.94, f32[1,2,64,1024]{3,2,1,0:T(8,128)S(1)} %bitcast.85, f32[1,2,64,1024]{3,2,1,0:T(8,128)S(1)} %bitcast.91, ...), kind=kLoop, calls=%fused_computation.46.clone.1 | loop fusion | flops 8552448 | bytes 12058624 | tf_op jit(solution)/shard_map/while/body/eval_jaxpr/add | solution.py:36
  62.1 3.2 %fusion.118 = f32[2,72,1024]{2,1,0:T(8,128)S(1)} fusion(f32[2,2,72,1024]{3,2,1,0:T(8,128)S(1)} %fusion.117, f32[4,2,80,1024]{3,2,1,0:T(8,128)S(1)} %pad_maximum_fusion.23, s32[2,512]{1,0:T(2,128)S(1)} %copy-done.17, f32[72,1024]{1,0:T(8,128)S(1)} %bitcast.103, f32[72,1024]{1,0:T(8,128)S(1)} %bitcast.99, f32[2,512]{1,0:T(2,128)S(1)} %get-tuple-element.864, ...), kind=kOutput, calls=%fused_computation.109.clone.1 | convolution fusion | flops 909246464 | bytes 2961696 | tf_op jit(solution)/shard_map/while/body/eval_jaxpr/szr,srx->szx/dot_general | solution.py:81
  65.4 2.4 fusion.121
  69.1 3.1 %fusion.122 = f32[2,64,1024]{2,1,0:T(8,128)S(1)} fusion(s32[2,512]{1,0:T(2,128)S(1)} %copy-done.17, f32[2,2,64,1024]{3,2,1,0:T(8,128)S(1)} %fusion.121, f32[2,64,1024]{2,1,0:T(8,128)S(1)} %get-tuple-element.904, f32[2,64,1024]{2,1,0:T(8,128)S(1)} %get-tuple-element.927, f32[64,1024]{1,0:T(8,128)S(1)} %copy-done.12, ...), kind=kOutput, calls=%fused_computation.39.clone.1 | convolution fusion | flops 808452096 | bytes 2633984 | tf_op jit(solution)/shard_map/while/body/eval_jaxpr/szr,srx->szx/dot_general | solution.py:81
  73.9 1.3 collective-permute-start
  75.2 4.9 %collective-permute-start.1 = (f32[4,2,8,1024]{3,2,1,0:T(8,128)}, f32[4,2,8,1024]{3,2,1,0:T(8,128)S(1)}, u32[]{:S(2)}, u32[]{:S(2)}) collective-permute-start(f32[4,2,8,1024]{3,2,1,0:T(8,128)} %get-tuple-element.863), channel_id=1, source_target_pairs={{0,1},{1,2},{2,3},{4,5},{5,6},{6,7},{8,9},{9,10},{10,11},{12,13},{... | collective-permute-start | bytes 786440 | tf_op jit(solution)/shard_map/while/body/eval_jaxpr/ppermute | solution.py:19
  82.8 1.6 collective-permute-done.1
  84.7 2.6 %fusion.117 = f32[2,2,72,1024]{3,2,1,0:T(8,128)S(1)} fusion(f32[2,2,72,1024]{3,2,1,0:T(8,128)S(1)} %slice.1057, f32[4,2,8,1024]{3,2,1,0:T(8,128)S(1)} %collective-permute-done.1, f32[1,2,64,1024]{3,2,1,0:T(8,128)S(1)} %bitcast.94, f32[1,2,64,1024]{3,2,1,0:T(8,128)S(1)} %bitcast.85, f32[1,2,64,1024]{3,2,1,0:T(8,128)S(1)} %bitcast.91, ...), kind=kLoop, calls=%fused_computation.46.clone.1 | loop fusion | flops 8552448 | bytes 12058624 | tf_op jit(solution)/shard_map/while/body/eval_jaxpr/add | solution.py:36
  88.3 3.2 %fusion.118 = f32[2,72,1024]{2,1,0:T(8,128)S(1)} fusion(f32[2,2,72,1024]{3,2,1,0:T(8,128)S(1)} %fusion.117, f32[4,2,80,1024]{3,2,1,0:T(8,128)S(1)} %pad_maximum_fusion.23, s32[2,512]{1,0:T(2,128)S(1)} %copy-done.17, f32[72,1024]{1,0:T(8,128)S(1)} %bitcast.103, f32[72,1024]{1,0:T(8,128)S(1)} %bitcast.99, f32[2,512]{1,0:T(2,128)S(1)} %get-tuple-element.864, ...), kind=kOutput, calls=%fused_computation.109.clone.1 | convolution fusion | flops 909246464 | bytes 2961696 | tf_op jit(solution)/shard_map/while/body/eval_jaxpr/szr,srx->szx/dot_general | solution.py:81
  91.6 2.4 fusion.121
  95.2 3.1 %fusion.122 = f32[2,64,1024]{2,1,0:T(8,128)S(1)} fusion(s32[2,512]{1,0:T(2,128)S(1)} %copy-done.17, f32[2,2,64,1024]{3,2,1,0:T(8,128)S(1)} %fusion.121, f32[2,64,1024]{2,1,0:T(8,128)S(1)} %get-tuple-element.904, f32[2,64,1024]{2,1,0:T(8,128)S(1)} %get-tuple-element.927, f32[64,1024]{1,0:T(8,128)S(1)} %copy-done.12, ...), kind=kOutput, calls=%fused_computation.39.clone.1 | convolution fusion | flops 808452096 | bytes 2633984 | tf_op jit(solution)/shard_map/while/body/eval_jaxpr/szr,srx->szx/dot_general | solution.py:81
  100.1 1.3 collective-permute-start
  101.4 4.9 %collective-permute-start.1 = (f32[4,2,8,1024]{3,2,1,0:T(8,128)}, f32[4,2,8,1024]{3,2,1,0:T(8,128)S(1)}, u32[]{:S(2)}, u32[]{:S(2)}) collective-permute-start(f32[4,2,8,1024]{3,2,1,0:T(8,128)} %get-tuple-element.863), channel_id=1, source_target_pairs={{0,1},{1,2},{2,3},{4,5},{5,6},{6,7},{8,9},{9,10},{10,11},{12,13},{... | collective-permute-start | bytes 786440 | tf_op jit(solution)/shard_map/while/body/eval_jaxpr/ppermute | solution.py:19
  108.9 1.6 collective-permute-done.1
  110.8 2.6 %fusion.117 = f32[2,2,72,1024]{3,2,1,0:T(8,128)S(1)} fusion(f32[2,2,72,1024]{3,2,1,0:T(8,128)S(1)} %slice.1057, f32[4,2,8,1024]{3,2,1,0:T(8,128)S(1)} %collective-permute-done.1, f32[1,2,64,1024]{3,2,1,0:T(8,128)S(1)} %bitcast.94, f32[1,2,64,1024]{3,2,1,0:T(8,128)S(1)} %bitcast.85, f32[1,2,64,1024]{3,2,1,0:T(8,128)S(1)} %bitcast.91, ...), kind=kLoop, calls=%fused_computation.46.clone.1 | loop fusion | flops 8552448 | bytes 12058624 | tf_op jit(solution)/shard_map/while/body/eval_jaxpr/add | solution.py:36
  114.4 3.2 %fusion.118 = f32[2,72,1024]{2,1,0:T(8,128)S(1)} fusion(f32[2,2,72,1024]{3,2,1,0:T(8,128)S(1)} %fusion.117, f32[4,2,80,1024]{3,2,1,0:T(8,128)S(1)} %pad_maximum_fusion.23, s32[2,512]{1,0:T(2,128)S(1)} %copy-done.17, f32[72,1024]{1,0:T(8,128)S(1)} %bitcast.103, f32[72,1024]{1,0:T(8,128)S(1)} %bitcast.99, f32[2,512]{1,0:T(2,128)S(1)} %get-tuple-element.864, ...), kind=kOutput, calls=%fused_computation.109.clone.1 | convolution fusion | flops 909246464 | bytes 2961696 | tf_op jit(solution)/shard_map/while/body/eval_jaxpr/szr,srx->szx/dot_general | solution.py:81
  117.8 2.4 fusion.121
  121.4 3.1 %fusion.122 = f32[2,64,1024]{2,1,0:T(8,128)S(1)} fusion(s32[2,512]{1,0:T(2,128)S(1)} %copy-done.17, f32[2,2,64,1024]{3,2,1,0:T(8,128)S(1)} %fusion.121, f32[2,64,1024]{2,1,0:T(8,128)S(1)} %get-tuple-element.904, f32[2,64,1024]{2,1,0:T(8,128)S(1)} %get-tuple-element.927, f32[64,1024]{1,0:T(8,128)S(1)} %copy-done.12, ...), kind=kOutput, calls=%fused_computation.39.clone.1 | convolution fusion | flops 808452096 | bytes 2633984 | tf_op jit(solution)/shard_map/while/body/eval_jaxpr/szr,srx->szx/dot_general | solution.py:81
  126.3 1.3 collective-permute-start
  127.6 4.9 %collective-permute-start.1 = (f32[4,2,8,1024]{3,2,1,0:T(8,128)}, f32[4,2,8,1024]{3,2,1,0:T(8,128)S(1)}, u32[]{:S(2)}, u32[]{:S(2)}) collective-permute-start(f32[4,2,8,1024]{3,2,1,0:T(8,128)} %get-tuple-element.863), channel_id=1, source_target_pairs={{0,1},{1,2},{2,3},{4,5},{5,6},{6,7},{8,9},{9,10},{10,11},{12,13},{... | collective-permute-start | bytes 786440 | tf_op jit(solution)/shard_map/while/body/eval_jaxpr/ppermute | solution.py:19
  135.1 1.6 collective-permute-done.1
  137.0 2.6 %fusion.117 = f32[2,2,72,1024]{3,2,1,0:T(8,128)S(1)} fusion(f32[2,2,72,1024]{3,2,1,0:T(8,128)S(1)} %slice.1057, f32[4,2,8,1024]{3,2,1,0:T(8,128)S(1)} %collective-permute-done.1, f32[1,2,64,1024]{3,2,1,0:T(8,128)S(1)} %bitcast.94, f32[1,2,64,1024]{3,2,1,0:T(8,128)S(1)} %bitcast.85, f32[1,2,64,1024]{3,2,1,0:T(8,128)S(1)} %bitcast.91, ...), kind=kLoop, calls=%fused_computation.46.clone.1 | loop fusion | flops 8552448 | bytes 12058624 | tf_op jit(solution)/shard_map/while/body/eval_jaxpr/add | solution.py:36
  140.6 3.2 %fusion.118 = f32[2,72,1024]{2,1,0:T(8,128)S(1)} fusion(f32[2,2,72,1024]{3,2,1,0:T(8,128)S(1)} %fusion.117, f32[4,2,80,1024]{3,2,1,0:T(8,128)S(1)} %pad_maximum_fusion.23, s32[2,512]{1,0:T(2,128)S(1)} %copy-done.17, f32[72,1024]{1,0:T(8,128)S(1)} %bitcast.103, f32[72,1024]{1,0:T(8,128)S(1)} %bitcast.99, f32[2,512]{1,0:T(2,128)S(1)} %get-tuple-element.864, ...), kind=kOutput, calls=%fused_computation.109.clone.1 | convolution fusion | flops 909246464 | bytes 2961696 | tf_op jit(solution)/shard_map/while/body/eval_jaxpr/szr,srx->szx/dot_general | solution.py:81
  143.9 2.4 fusion.121
  147.6 3.1 %fusion.122 = f32[2,64,1024]{2,1,0:T(8,128)S(1)} fusion(s32[2,512]{1,0:T(2,128)S(1)} %copy-done.17, f32[2,2,64,1024]{3,2,1,0:T(8,128)S(1)} %fusion.121, f32[2,64,1024]{2,1,0:T(8,128)S(1)} %get-tuple-element.904, f32[2,64,1024]{2,1,0:T(8,128)S(1)} %get-tuple-element.927, f32[64,1024]{1,0:T(8,128)S(1)} %copy-done.12, ...), kind=kOutput, calls=%fused_computation.39.clone.1 | convolution fusion | flops 808452096 | bytes 2633984 | tf_op jit(solution)/shard_map/while/body/eval_jaxpr/szr,srx->szx/dot_general | solution.py:81
  152.4 1.3 collective-permute-start
  153.7 4.9 %collective-permute-start.1 = (f32[4,2,8,1024]{3,2,1,0:T(8,128)}, f32[4,2,8,1024]{3,2,1,0:T(8,128)S(1)}, u32[]{:S(2)}, u32[]{:S(2)}) collective-permute-start(f32[4,2,8,1024]{3,2,1,0:T(8,128)} %get-tuple-element.863), channel_id=1, source_target_pairs={{0,1},{1,2},{2,3},{4,5},{5,6},{6,7},{8,9},{9,10},{10,11},{12,13},{... | collective-permute-start | bytes 786440 | tf_op jit(solution)/shard_map/while/body/eval_jaxpr/ppermute | solution.py:19
  161.3 1.6 collective-permute-done.1
  163.2 2.6 %fusion.117 = f32[2,2,72,1024]{3,2,1,0:T(8,128)S(1)} fusion(f32[2,2,72,1024]{3,2,1,0:T(8,128)S(1)} %slice.1057, f32[4,2,8,1024]{3,2,1,0:T(8,128)S(1)} %collective-permute-done.1, f32[1,2,64,1024]{3,2,1,0:T(8,128)S(1)} %bitcast.94, f32[1,2,64,1024]{3,2,1,0:T(8,128)S(1)} %bitcast.85, f32[1,2,64,1024]{3,2,1,0:T(8,128)S(1)} %bitcast.91, ...), kind=kLoop, calls=%fused_computation.46.clone.1 | loop fusion | flops 8552448 | bytes 12058624 | tf_op jit(solution)/shard_map/while/body/eval_jaxpr/add | solution.py:36
  166.8 3.2 %fusion.118 = f32[2,72,1024]{2,1,0:T(8,128)S(1)} fusion(f32[2,2,72,1024]{3,2,1,0:T(8,128)S(1)} %fusion.117, f32[4,2,80,1024]{3,2,1,0:T(8,128)S(1)} %pad_maximum_fusion.23, s32[2,512]{1,0:T(2,128)S(1)} %copy-done.17, f32[72,1024]{1,0:T(8,128)S(1)} %bitcast.103, f32[72,1024]{1,0:T(8,128)S(1)} %bitcast.99, f32[2,512]{1,0:T(2,128)S(1)} %get-tuple-element.864, ...), kind=kOutput, calls=%fused_computation.109.clone.1 | convolution fusion | flops 909246464 | bytes 2961696 | tf_op jit(solution)/shard_map/while/body/eval_jaxpr/szr,srx->szx/dot_general | solution.py:81
  170.1 2.4 fusion.121
  173.8 3.1 %fusion.122 = f32[2,64,1024]{2,1,0:T(8,128)S(1)} fusion(s32[2,512]{1,0:T(2,128)S(1)} %copy-done.17, f32[2,2,64,1024]{3,2,1,0:T(8,128)S(1)} %fusion.121, f32[2,64,1024]{2,1,0:T(8,128)S(1)} %get-tuple-element.904, f32[2,64,1024]{2,1,0:T(8,128)S(1)} %get-tuple-element.927, f32[64,1024]{1,0:T(8,128)S(1)} %copy-done.12, ...), kind=kOutput, calls=%fused_computation.39.clone.1 | convolution fusion | flops 808452096 | bytes 2633984 | tf_op jit(solution)/shard_map/while/body/eval_jaxpr/szr,srx->szx/dot_general | solution.py:81
  178.6 1.3 collective-permute-start
  179.9 4.9 %collective-permute-start.1 = (f32[4,2,8,1024]{3,2,1,0:T(8,128)}, f32[4,2,8,1024]{3,2,1,0:T(8,128)S(1)}, u32[]{:S(2)}, u32[]{:S(2)}) collective-permute-start(f32[4,2,8,1024]{3,2,1,0:T(8,128)} %get-tuple-element.863), channel_id=1, source_target_pairs={{0,1},{1,2},{2,3},{4,5},{5,6},{6,7},{8,9},{9,10},{10,11},{12,13},{... | collective-permute-start | bytes 786440 | tf_op jit(solution)/shard_map/while/body/eval_jaxpr/ppermute | solution.py:19
  187.4 1.6 collective-permute-done.1
  189.4 2.6 %fusion.117 = f32[2,2,72,1024]{3,2,1,0:T(8,128)S(1)} fusion(f32[2,2,72,1024]{3,2,1,0:T(8,128)S(1)} %slice.1057, f32[4,2,8,1024]{3,2,1,0:T(8,128)S(1)} %collective-permute-done.1, f32[1,2,64,1024]{3,2,1,0:T(8,128)S(1)} %bitcast.94, f32[1,2,64,1024]{3,2,1,0:T(8,128)S(1)} %bitcast.85, f32[1,2,64,1024]{3,2,1,0:T(8,128)S(1)} %bitcast.91, ...), kind=kLoop, calls=%fused_computation.46.clone.1 | loop fusion | flops 8552448 | bytes 12058624 | tf_op jit(solution)/shard_map/while/body/eval_jaxpr/add | solution.py:36
  193.0 3.2 %fusion.118 = f32[2,72,1024]{2,1,0:T(8,128)S(1)} fusion(f32[2,2,72,1024]{3,2,1,0:T(8,128)S(1)} %fusion.117, f32[4,2,80,1024]{3,2,1,0:T(8,128)S(1)} %pad_maximum_fusion.23, s32[2,512]{1,0:T(2,128)S(1)} %copy-done.17, f32[72,1024]{1,0:T(8,128)S(1)} %bitcast.103, f32[72,1024]{1,0:T(8,128)S(1)} %bitcast.99, f32[2,512]{1,0:T(2,128)S(1)} %get-tuple-element.864, ...), kind=kOutput, calls=%fused_computation.109.clone.1 | convolution fusion | flops 909246464 | bytes 2961696 | tf_op jit(solution)/shard_map/while/body/eval_jaxpr/szr,srx->szx/dot_general | solution.py:81
  196.3 2.4 fusion.121
  199.9 3.1 %fusion.122 = f32[2,64,1024]{2,1,0:T(8,128)S(1)} fusion(s32[2,512]{1,0:T(2,128)S(1)} %copy-done.17, f32[2,2,64,1024]{3,2,1,0:T(8,128)S(1)} %fusion.121, f32[2,64,1024]{2,1,0:T(8,128)S(1)} %get-tuple-element.904, f32[2,64,1024]{2,1,0:T(8,128)S(1)} %get-tuple-element.927, f32[64,1024]{1,0:T(8,128)S(1)} %copy-done.12, ...), kind=kOutput, calls=%fused_computation.39.clone.1 | convolution fusion | flops 808452096 | bytes 2633984 | tf_op jit(solution)/shard_map/while/body/eval_jaxpr/szr,srx->szx/dot_general | solution.py:81
  204.8 1.3 collective-permute-start
  206.1 4.9 %collective-permute-start.1 = (f32[4,2,8,1024]{3,2,1,0:T(8,128)}, f32[4,2,8,1024]{3,2,1,0:T(8,128)S(1)}, u32[]{:S(2)}, u32[]{:S(2)}) collective-permute-start(f32[4,2,8,1024]{3,2,1,0:T(8,128)} %get-tuple-element.863), channel_id=1, source_target_pairs={{0,1},{1,2},{2,3},{4,5},{5,6},{6,7},{8,9},{9,10},{10,11},{12,13},{... | collective-permute-start | bytes 786440 | tf_op jit(solution)/shard_map/while/body/eval_jaxpr/ppermute | solution.py:19
  213.6 1.6 collective-permute-done.1
  215.5 2.6 %fusion.117 = f32[2,2,72,1024]{3,2,1,0:T(8,128)S(1)} fusion(f32[2,2,72,1024]{3,2,1,0:T(8,128)S(1)} %slice.1057, f32[4,2,8,1024]{3,2,1,0:T(8,128)S(1)} %collective-permute-done.1, f32[1,2,64,1024]{3,2,1,0:T(8,128)S(1)} %bitcast.94, f32[1,2,64,1024]{3,2,1,0:T(8,128)S(1)} %bitcast.85, f32[1,2,64,1024]{3,2,1,0:T(8,128)S(1)} %bitcast.91, ...), kind=kLoop, calls=%fused_computation.46.clone.1 | loop fusion | flops 8552448 | bytes 12058624 | tf_op jit(solution)/shard_map/while/body/eval_jaxpr/add | solution.py:36
  219.1 3.2 %fusion.118 = f32[2,72,1024]{2,1,0:T(8,128)S(1)} fusion(f32[2,2,72,1024]{3,2,1,0:T(8,128)S(1)} %fusion.117, f32[4,2,80,1024]{3,2,1,0:T(8,128)S(1)} %pad_maximum_fusion.23, s32[2,512]{1,0:T(2,128)S(1)} %copy-done.17, f32[72,1024]{1,0:T(8,128)S(1)} %bitcast.103, f32[72,1024]{1,0:T(8,128)S(1)} %bitcast.99, f32[2,512]{1,0:T(2,128)S(1)} %get-tuple-element.864, ...), kind=kOutput, calls=%fused_computation.109.clone.1 | convolution fusion | flops 909246464 | bytes 2961696 | tf_op jit(solution)/shard_map/while/body/eval_jaxpr/szr,srx->szx/dot_general | solution.py:81
  222.4 2.4 fusion.121
  226.1 3.1 %fusion.122 = f32[2,64,1024]{2,1,0:T(8,128)S(1)} fusion(s32[2,512]{1,0:T(2,128)S(1)} %copy-done.17, f32[2,2,64,1024]{3,2,1,0:T(8,128)S(1)} %fusion.121, f32[2,64,1024]{2,1,0:T(8,128)S(1)} %get-tuple-element.904, f32[2,64,1024]{2,1,0:T(8,128)S(1)} %get-tuple-element.927, f32[64,1024]{1,0:T(8,128)S(1)} %copy-done.12, ...), kind=kOutput, calls=%fused_computation.39.clone.1 | convolution fusion | flops 808452096 | bytes 2633984 | tf_op jit(solution)/shard_map/while/body/eval_jaxpr/szr,srx->szx/dot_general | solution.py:81
  230.2 19.8 %all-gather.3.cloned.1.call-done = f32[256,1024]{1,0:T(8,128)} async-done(((f32[64,1024]{1,0:T(8,128)}), f32[256,1024]{1,0:T(8,128)}) %all-gather.3.cloned.1.call-update) | async-done | bytes 1048592 | tf_op jit(solution)/shard_map/all_gather | solution.py:143
  250.0 1.3 reduce_sum.47
  (371 shorter events, 57.8 us)
Async XLA Ops:
  7.2 242.8 %all-gather.3.cloned.1.call-start = ((), (), s32[]{:S(2)}) async-start(), calls=%async_computation | async-start | bytes 1310720 | tf_op jit(solution)/shard_map/all_gather | solution.py:143
  7.2 1.7 copy-start.7
  7.2 8.2 %copy-start.13 = (f32[2,16,512]{2,1,0:T(8,128)S(1)}, f32[2,16,512]{2,1,0:T(8,128)}, u32[]{:S(2)}) copy-start(f32[2,16,512]{2,1,0:T(8,128)} %param.21) | copy-start | bytes 196612
  8.2 12.9 %copy-start.6 = (f32[2,64,1024]{2,1,0:T(8,128)S(1)}, f32[2,64,1024]{2,1,0:T(8,128)}, u32[]{:S(2)}) copy-start(f32[2,64,1024]{2,1,0:T(8,128)} %param.19) | copy-start | bytes 1572868
  8.9 12.1 %copy-start = (f32[256]{0:T(256)S(1)}, f32[256]{0:T(256)}, u32[]{:S(2)}) copy-start(f32[256]{0:T(256)} %param.22) | copy-start | bytes 3076
  8.9 12.1 %copy-start.1 = (f32[2,64,1024]{2,1,0:T(8,128)S(1)}, f32[2,64,1024]{2,1,0:T(8,128)}, u32[]{:S(2)}) copy-start(f32[2,64,1024]{2,1,0:T(8,128)} %param.17) | copy-start | bytes 1572868
  8.9 12.1 %copy-start.3 = (f32[2,64,1024]{2,1,0:T(8,128)S(1)}, f32[2,64,1024]{2,1,0:T(8,128)}, u32[]{:S(2)}) copy-start(f32[2,64,1024]{2,1,0:T(8,128)} %param.18) | copy-start | bytes 1572868
  8.9 12.1 %copy-start.5 = (f32[2,64,1024]{2,1,0:T(8,128)S(1)}, f32[2,64,1024]{2,1,0:T(8,128)}, u32[]{:S(2)}) copy-start(f32[2,64,1024]{2,1,0:T(8,128)} %param.20) | copy-start | bytes 1572868
  8.9 12.1 %copy-start.14 = (s32[2]{0:T(128)S(1)}, s32[2]{0:T(128)}, u32[]{:S(2)}) copy-start(s32[2]{0:T(128)} %param.27) | copy-start | bytes 28
  8.9 12.1 %copy-start.15 = (s32[2]{0:T(128)S(1)}, s32[2]{0:T(128)}, u32[]{:S(2)}) copy-start(s32[2]{0:T(128)} %param.24) | copy-start | bytes 28
  8.9 12.1 %copy-start.16 = (s32[2,512]{1,0:T(2,128)S(1)}, s32[2,512]{1,0:T(2,128)}, u32[]{:S(2)}) copy-start(s32[2,512]{1,0:T(2,128)} %param.25) | copy-start | bytes 12292
  9.0 12.1 %copy-start.18 = (s32[2]{0:T(128)S(1)}, s32[2]{0:T(128)}, u32[]{:S(2)}) copy-start(s32[2]{0:T(128)} %param.23) | copy-start | bytes 28
  9.0 7.0 %collective-permute-start.2 = (f32[2,8,1024]{2,1,0:T(8,128)S(1)}, f32[2,8,1024]{2,1,0:T(8,128)S(1)}, u32[]{:S(2)}, u32[]{:S(2)}) collective-permute-start(f32[2,8,1024]{2,1,0:T(8,128)S(1)} %get-tuple-element.729), channel_id=1, source_target_pairs={{0,1},{1,2},{2,3},{4,5},{5,6},{6,7},{8,9},{9,10},{10,11},{12,13},{... | collective-permute-start | bytes 196616 | tf_op jit(solution)/shard_map/ppermute | solution.py:19
  14.1 6.2 %collective-permute-start.3 = (f32[2,8,1024]{2,1,0:T(8,128)S(1)}, f32[2,8,1024]{2,1,0:T(8,128)S(1)}, u32[]{:S(2)}, u32[]{:S(2)}) collective-permute-start(f32[2,8,1024]{2,1,0:T(8,128)S(1)} %get-tuple-element.730), channel_id=1, source_target_pairs={{1,0},{2,1},{3,2},{5,4},{6,5},{7,6},{9,8},{10,9},{11,10},{13,12},{... | collective-permute-start | bytes 196616 | tf_op jit(solution)/shard_map/ppermute | solution.py:21
  21.9 8.7 %collective-permute-start = (f32[4,2,8,1024]{3,2,1,0:T(8,128)}, f32[4,2,8,1024]{3,2,1,0:T(8,128)S(1)}, u32[]{:S(2)}, u32[]{:S(2)}) collective-permute-start(f32[4,2,8,1024]{3,2,1,0:T(8,128)} %get-tuple-element.862), channel_id=1, source_target_pairs={{1,0},{2,1},{3,2},{5,4},{6,5},{7,6},{9,8},{10,9},{11,10},{13,12},{... | collective-permute-start | bytes 786440 | tf_op jit(solution)/shard_map/while/body/eval_jaxpr/ppermute | solution.py:21
  23.2 8.7 %collective-permute-start.1 = (f32[4,2,8,1024]{3,2,1,0:T(8,128)}, f32[4,2,8,1024]{3,2,1,0:T(8,128)S(1)}, u32[]{:S(2)}, u32[]{:S(2)}) collective-permute-start(f32[4,2,8,1024]{3,2,1,0:T(8,128)} %get-tuple-element.863), channel_id=1, source_target_pairs={{0,1},{1,2},{2,3},{4,5},{5,6},{6,7},{8,9},{9,10},{10,11},{12,13},{... | collective-permute-start | bytes 786440 | tf_op jit(solution)/shard_map/while/body/eval_jaxpr/ppermute | solution.py:19
  35.0 1.0 copy-start.10
  35.0 1.0 copy-start.17
  42.9 3.1 %copy-start.8 = (f32[64,1024]{1,0:T(8,128)S(1)}, f32[64,1024]{1,0:T(8,128)}, u32[]{:S(2)}) copy-start(f32[64,1024]{1,0:T(8,128)} %get-tuple-element.905) | copy-start | bytes 786436 | tf_op jit(solution)/shard_map/while
  42.9 4.0 %copy-start.19 = (s32[2]{0:T(128)S(1)}, s32[2]{0:T(128)}, u32[]{:S(2)}) copy-start(s32[2]{0:T(128)} %get-tuple-element.982) | copy-start | bytes 28 | tf_op jit(solution)/shard_map/while
  47.8 8.8 %collective-permute-start = (f32[4,2,8,1024]{3,2,1,0:T(8,128)}, f32[4,2,8,1024]{3,2,1,0:T(8,128)S(1)}, u32[]{:S(2)}, u32[]{:S(2)}) collective-permute-start(f32[4,2,8,1024]{3,2,1,0:T(8,128)} %get-tuple-element.862), channel_id=1, source_target_pairs={{1,0},{2,1},{3,2},{5,4},{6,5},{7,6},{9,8},{10,9},{11,10},{13,12},{... | collective-permute-start | bytes 786440 | tf_op jit(solution)/shard_map/while/body/eval_jaxpr/ppermute | solution.py:21
  49.0 9.1 %collective-permute-start.1 = (f32[4,2,8,1024]{3,2,1,0:T(8,128)}, f32[4,2,8,1024]{3,2,1,0:T(8,128)S(1)}, u32[]{:S(2)}, u32[]{:S(2)}) collective-permute-start(f32[4,2,8,1024]{3,2,1,0:T(8,128)} %get-tuple-element.863), channel_id=1, source_target_pairs={{0,1},{1,2},{2,3},{4,5},{5,6},{6,7},{8,9},{9,10},{10,11},{12,13},{... | collective-permute-start | bytes 786440 | tf_op jit(solution)/shard_map/while/body/eval_jaxpr/ppermute | solution.py:19
  61.1 1.0 copy-start.10
  61.1 1.0 copy-start.17
  69.1 3.1 %copy-start.8 = (f32[64,1024]{1,0:T(8,128)S(1)}, f32[64,1024]{1,0:T(8,128)}, u32[]{:S(2)}) copy-start(f32[64,1024]{1,0:T(8,128)} %get-tuple-element.905) | copy-start | bytes 786436 | tf_op jit(solution)/shard_map/while
  69.1 4.0 %copy-start.19 = (s32[2]{0:T(128)S(1)}, s32[2]{0:T(128)}, u32[]{:S(2)}) copy-start(s32[2]{0:T(128)} %get-tuple-element.982) | copy-start | bytes 28 | tf_op jit(solution)/shard_map/while
  73.9 8.8 %collective-permute-start = (f32[4,2,8,1024]{3,2,1,0:T(8,128)}, f32[4,2,8,1024]{3,2,1,0:T(8,128)S(1)}, u32[]{:S(2)}, u32[]{:S(2)}) collective-permute-start(f32[4,2,8,1024]{3,2,1,0:T(8,128)} %get-tuple-element.862), channel_id=1, source_target_pairs={{1,0},{2,1},{3,2},{5,4},{6,5},{7,6},{9,8},{10,9},{11,10},{13,12},{... | collective-permute-start | bytes 786440 | tf_op jit(solution)/shard_map/while/body/eval_jaxpr/ppermute | solution.py:21
  75.2 9.1 %collective-permute-start.1 = (f32[4,2,8,1024]{3,2,1,0:T(8,128)}, f32[4,2,8,1024]{3,2,1,0:T(8,128)S(1)}, u32[]{:S(2)}, u32[]{:S(2)}) collective-permute-start(f32[4,2,8,1024]{3,2,1,0:T(8,128)} %get-tuple-element.863), channel_id=1, source_target_pairs={{0,1},{1,2},{2,3},{4,5},{5,6},{6,7},{8,9},{9,10},{10,11},{12,13},{... | collective-permute-start | bytes 786440 | tf_op jit(solution)/shard_map/while/body/eval_jaxpr/ppermute | solution.py:19
  87.3 1.0 copy-start.10
  87.3 1.0 copy-start.17
  95.2 3.1 %copy-start.8 = (f32[64,1024]{1,0:T(8,128)S(1)}, f32[64,1024]{1,0:T(8,128)}, u32[]{:S(2)}) copy-start(f32[64,1024]{1,0:T(8,128)} %get-tuple-element.905) | copy-start | bytes 786436 | tf_op jit(solution)/shard_map/while
  95.2 4.0 %copy-start.19 = (s32[2]{0:T(128)S(1)}, s32[2]{0:T(128)}, u32[]{:S(2)}) copy-start(s32[2]{0:T(128)} %get-tuple-element.982) | copy-start | bytes 28 | tf_op jit(solution)/shard_map/while
  100.1 8.8 %collective-permute-start = (f32[4,2,8,1024]{3,2,1,0:T(8,128)}, f32[4,2,8,1024]{3,2,1,0:T(8,128)S(1)}, u32[]{:S(2)}, u32[]{:S(2)}) collective-permute-start(f32[4,2,8,1024]{3,2,1,0:T(8,128)} %get-tuple-element.862), channel_id=1, source_target_pairs={{1,0},{2,1},{3,2},{5,4},{6,5},{7,6},{9,8},{10,9},{11,10},{13,12},{... | collective-permute-start | bytes 786440 | tf_op jit(solution)/shard_map/while/body/eval_jaxpr/ppermute | solution.py:21
  101.4 9.1 %collective-permute-start.1 = (f32[4,2,8,1024]{3,2,1,0:T(8,128)}, f32[4,2,8,1024]{3,2,1,0:T(8,128)S(1)}, u32[]{:S(2)}, u32[]{:S(2)}) collective-permute-start(f32[4,2,8,1024]{3,2,1,0:T(8,128)} %get-tuple-element.863), channel_id=1, source_target_pairs={{0,1},{1,2},{2,3},{4,5},{5,6},{6,7},{8,9},{9,10},{10,11},{12,13},{... | collective-permute-start | bytes 786440 | tf_op jit(solution)/shard_map/while/body/eval_jaxpr/ppermute | solution.py:19
  113.5 1.0 copy-start.10
  113.5 1.0 copy-start.17
  121.4 3.1 %copy-start.8 = (f32[64,1024]{1,0:T(8,128)S(1)}, f32[64,1024]{1,0:T(8,128)}, u32[]{:S(2)}) copy-start(f32[64,1024]{1,0:T(8,128)} %get-tuple-element.905) | copy-start | bytes 786436 | tf_op jit(solution)/shard_map/while
  121.4 4.0 %copy-start.19 = (s32[2]{0:T(128)S(1)}, s32[2]{0:T(128)}, u32[]{:S(2)}) copy-start(s32[2]{0:T(128)} %get-tuple-element.982) | copy-start | bytes 28 | tf_op jit(solution)/shard_map/while
  126.3 8.8 %collective-permute-start = (f32[4,2,8,1024]{3,2,1,0:T(8,128)}, f32[4,2,8,1024]{3,2,1,0:T(8,128)S(1)}, u32[]{:S(2)}, u32[]{:S(2)}) collective-permute-start(f32[4,2,8,1024]{3,2,1,0:T(8,128)} %get-tuple-element.862), channel_id=1, source_target_pairs={{1,0},{2,1},{3,2},{5,4},{6,5},{7,6},{9,8},{10,9},{11,10},{13,12},{... | collective-permute-start | bytes 786440 | tf_op jit(solution)/shard_map/while/body/eval_jaxpr/ppermute | solution.py:21
  127.6 9.1 %collective-permute-start.1 = (f32[4,2,8,1024]{3,2,1,0:T(8,128)}, f32[4,2,8,1024]{3,2,1,0:T(8,128)S(1)}, u32[]{:S(2)}, u32[]{:S(2)}) collective-permute-start(f32[4,2,8,1024]{3,2,1,0:T(8,128)} %get-tuple-element.863), channel_id=1, source_target_pairs={{0,1},{1,2},{2,3},{4,5},{5,6},{6,7},{8,9},{9,10},{10,11},{12,13},{... | collective-permute-start | bytes 786440 | tf_op jit(solution)/shard_map/while/body/eval_jaxpr/ppermute | solution.py:19
  139.6 1.0 copy-start.10
  139.7 1.0 copy-start.17
  147.6 3.1 %copy-start.8 = (f32[64,1024]{1,0:T(8,128)S(1)}, f32[64,1024]{1,0:T(8,128)}, u32[]{:S(2)}) copy-start(f32[64,1024]{1,0:T(8,128)} %get-tuple-element.905) | copy-start | bytes 786436 | tf_op jit(solution)/shard_map/while
  147.6 4.0 %copy-start.19 = (s32[2]{0:T(128)S(1)}, s32[2]{0:T(128)}, u32[]{:S(2)}) copy-start(s32[2]{0:T(128)} %get-tuple-element.982) | copy-start | bytes 28 | tf_op jit(solution)/shard_map/while
  152.4 8.8 %collective-permute-start = (f32[4,2,8,1024]{3,2,1,0:T(8,128)}, f32[4,2,8,1024]{3,2,1,0:T(8,128)S(1)}, u32[]{:S(2)}, u32[]{:S(2)}) collective-permute-start(f32[4,2,8,1024]{3,2,1,0:T(8,128)} %get-tuple-element.862), channel_id=1, source_target_pairs={{1,0},{2,1},{3,2},{5,4},{6,5},{7,6},{9,8},{10,9},{11,10},{13,12},{... | collective-permute-start | bytes 786440 | tf_op jit(solution)/shard_map/while/body/eval_jaxpr/ppermute | solution.py:21
  153.7 9.1 %collective-permute-start.1 = (f32[4,2,8,1024]{3,2,1,0:T(8,128)}, f32[4,2,8,1024]{3,2,1,0:T(8,128)S(1)}, u32[]{:S(2)}, u32[]{:S(2)}) collective-permute-start(f32[4,2,8,1024]{3,2,1,0:T(8,128)} %get-tuple-element.863), channel_id=1, source_target_pairs={{0,1},{1,2},{2,3},{4,5},{5,6},{6,7},{8,9},{9,10},{10,11},{12,13},{... | collective-permute-start | bytes 786440 | tf_op jit(solution)/shard_map/while/body/eval_jaxpr/ppermute | solution.py:19
  165.8 1.0 copy-start.10
  165.8 1.0 copy-start.17
  173.8 3.1 %copy-start.8 = (f32[64,1024]{1,0:T(8,128)S(1)}, f32[64,1024]{1,0:T(8,128)}, u32[]{:S(2)}) copy-start(f32[64,1024]{1,0:T(8,128)} %get-tuple-element.905) | copy-start | bytes 786436 | tf_op jit(solution)/shard_map/while
  173.8 4.0 %copy-start.19 = (s32[2]{0:T(128)S(1)}, s32[2]{0:T(128)}, u32[]{:S(2)}) copy-start(s32[2]{0:T(128)} %get-tuple-element.982) | copy-start | bytes 28 | tf_op jit(solution)/shard_map/while
  178.6 8.8 %collective-permute-start = (f32[4,2,8,1024]{3,2,1,0:T(8,128)}, f32[4,2,8,1024]{3,2,1,0:T(8,128)S(1)}, u32[]{:S(2)}, u32[]{:S(2)}) collective-permute-start(f32[4,2,8,1024]{3,2,1,0:T(8,128)} %get-tuple-element.862), channel_id=1, source_target_pairs={{1,0},{2,1},{3,2},{5,4},{6,5},{7,6},{9,8},{10,9},{11,10},{13,12},{... | collective-permute-start | bytes 786440 | tf_op jit(solution)/shard_map/while/body/eval_jaxpr/ppermute | solution.py:21
  179.9 9.1 %collective-permute-start.1 = (f32[4,2,8,1024]{3,2,1,0:T(8,128)}, f32[4,2,8,1024]{3,2,1,0:T(8,128)S(1)}, u32[]{:S(2)}, u32[]{:S(2)}) collective-permute-start(f32[4,2,8,1024]{3,2,1,0:T(8,128)} %get-tuple-element.863), channel_id=1, source_target_pairs={{0,1},{1,2},{2,3},{4,5},{5,6},{6,7},{8,9},{9,10},{10,11},{12,13},{... | collective-permute-start | bytes 786440 | tf_op jit(solution)/shard_map/while/body/eval_jaxpr/ppermute | solution.py:19
  192.0 1.0 copy-start.10
  192.0 1.0 copy-start.17
  199.9 3.1 %copy-start.8 = (f32[64,1024]{1,0:T(8,128)S(1)}, f32[64,1024]{1,0:T(8,128)}, u32[]{:S(2)}) copy-start(f32[64,1024]{1,0:T(8,128)} %get-tuple-element.905) | copy-start | bytes 786436 | tf_op jit(solution)/shard_map/while
  199.9 4.0 %copy-start.19 = (s32[2]{0:T(128)S(1)}, s32[2]{0:T(128)}, u32[]{:S(2)}) copy-start(s32[2]{0:T(128)} %get-tuple-element.982) | copy-start | bytes 28 | tf_op jit(solution)/shard_map/while
  204.8 8.8 %collective-permute-start = (f32[4,2,8,1024]{3,2,1,0:T(8,128)}, f32[4,2,8,1024]{3,2,1,0:T(8,128)S(1)}, u32[]{:S(2)}, u32[]{:S(2)}) collective-permute-start(f32[4,2,8,1024]{3,2,1,0:T(8,128)} %get-tuple-element.862), channel_id=1, source_target_pairs={{1,0},{2,1},{3,2},{5,4},{6,5},{7,6},{9,8},{10,9},{11,10},{13,12},{... | collective-permute-start | bytes 786440 | tf_op jit(solution)/shard_map/while/body/eval_jaxpr/ppermute | solution.py:21
  206.1 9.1 %collective-permute-start.1 = (f32[4,2,8,1024]{3,2,1,0:T(8,128)}, f32[4,2,8,1024]{3,2,1,0:T(8,128)S(1)}, u32[]{:S(2)}, u32[]{:S(2)}) collective-permute-start(f32[4,2,8,1024]{3,2,1,0:T(8,128)} %get-tuple-element.863), channel_id=1, source_target_pairs={{0,1},{1,2},{2,3},{4,5},{5,6},{6,7},{8,9},{9,10},{10,11},{12,13},{... | collective-permute-start | bytes 786440 | tf_op jit(solution)/shard_map/while/body/eval_jaxpr/ppermute | solution.py:19
  218.2 1.0 copy-start.10
  218.2 1.0 copy-start.17
  226.1 3.1 %copy-start.8 = (f32[64,1024]{1,0:T(8,128)S(1)}, f32[64,1024]{1,0:T(8,128)}, u32[]{:S(2)}) copy-start(f32[64,1024]{1,0:T(8,128)} %get-tuple-element.905) | copy-start | bytes 786436 | tf_op jit(solution)/shard_map/while
  226.1 4.0 %copy-start.19 = (s32[2]{0:T(128)S(1)}, s32[2]{0:T(128)}, u32[]{:S(2)}) copy-start(s32[2]{0:T(128)} %get-tuple-element.982) | copy-start | bytes 28 | tf_op jit(solution)/shard_map/while
  230.1 21.9 %copy-start.2 = (f32[2,64,1024]{2,1,0:T(8,128)}, f32[2,64,1024]{2,1,0:T(8,128)S(1)}, u32[]{:S(2)}) copy-start(f32[2,64,1024]{2,1,0:T(8,128)S(1)} %get-tuple-element.960) | copy-start | bytes 1572868
  230.1 21.9 %copy-start.4 = (f32[2,64,1024]{2,1,0:T(8,128)}, f32[2,64,1024]{2,1,0:T(8,128)S(1)}, u32[]{:S(2)}) copy-start(f32[2,64,1024]{2,1,0:T(8,128)S(1)} %get-tuple-element.962) | copy-start | bytes 1572868
  (49 other events, 38.4 us)
Sparse Core Ops, SparseCore 0:
  230.3 19.6 all-gather.2
